TPU v7x, 32 devices: a whole 2x2x4 slice. The times are simulated.
32 devices in a mesh: groups: 2 (over x), az: 16 (over z, y, core).
Axes of the slice: x: 2, y: 2, z: 4, core: 2. Of those that a mesh axis runs over, the one named last changes fastest.
Arguments:
- raw_first: bfloat16 [4, 8192, 8192], P('groups', 'az'), parts along dimension 0, may hold values from -6 to 6
- raw_second: bfloat16 [4, 8192, 8192], P('groups', 'az'), parts along dimension 0, may hold values from -6 to 6
- offsets: int32 [4], P('groups'), parts along dimension 0, may hold values from -16 to 16
- chirp_lengths: int32 [4], P('groups'), parts along dimension 0, may hold values from 256 to 2048
Outputs:
- interferogram: float32 [4, 1024, 8192], P('groups', 'az'), parts along dimension 0
- coherence: float32 [2048, 8192], P(('groups', 'az')), parts along dimension 0
There are 2 independent parts, one for each index of `groups`. A program takes and returns all parts, laid end to end along the dimension named above; each array names one. Nothing has to cross between parts.
Inputs may be any that keep to these rules, and one draw needn't show every extreme that they name: offsets[0] shifts azimuth lines, offsets[1] range bins. chirp_lengths[0] is the range chirp, chirp_lengths[1] the azimuth chirp.
All inputs are finite; a program needn't handle non-finite values.
Results may differ from a plain program's by a relative error of at most 0.0003.
Values sent between devices are 32-bit elements; how exact they have to be, the bound alone decides.
A program may use at most 256 MiB of HBM per device.

v0:
```python
import functools
import math

import jax
import jax.numpy as jnp
from jax import lax
from jax.experimental import pallas as pl
from jax.experimental.pallas import tpu as pltpu
from jax.sharding import PartitionSpec as P

WINDOW = 1024
MAXSHIFT = 16
LANES = 128
TILE = 256
VMEM_BYTES = 60 * 1024 * 1024


along_forms = (
    ("rij", "ik", "rkj"),
    ("rkj", "jl", "rkl"),
    ("rkl", "jl", "rkj"),
    ("rkj", "ik", "rij"),
)


def padded_2(block, sides, width):
    for axis, dim in sides:
        count = lax.axis_size(axis)
        forward = [(i, i + 1) for i in range(count - 1)]
        backward = [(target, source) for source, target in forward]
        low = lax.ppermute(
            lax.slice_in_dim(block, block.shape[dim] - width, None, axis=dim), axis, forward
        )
        high = lax.ppermute(lax.slice_in_dim(block, 0, width, axis=dim), axis, backward)
        block = jnp.concatenate([low, block, high], axis=dim)
    return block


def chirp(length, samples_all):
    sample = jnp.arange(samples_all, dtype=jnp.int32)
    offset = 2 * sample - length
    period = 8 * length
    numerator = jnp.mod(offset * offset, period)
    angles = jnp.pi * numerator.astype(jnp.float32) / (4 * length).astype(jnp.float32)
    amplitude = jnp.where(sample < length, 1.0 / jnp.sqrt(length.astype(jnp.float32)), 0.0)
    return (amplitude * jnp.cos(angles), amplitude * jnp.sin(angles))


def roots(rows_count, cols_count, period):
    product = lax.broadcasted_iota(jnp.int32, (rows_count, cols_count), 0) * lax.broadcasted_iota(
        jnp.int32, (rows_count, cols_count), 1
    )
    angles = -2.0 * math.pi / period * jnp.mod(product, period).astype(jnp.float32)
    return (jnp.cos(angles), jnp.sin(angles))


def tables(length):
    right_size = LANES
    left_size = length // right_size
    entries = (
        roots(left_size, left_size, left_size)
        + roots(right_size, right_size, right_size)
        + roots(left_size, right_size, length)
    )
    return (entries, left_size, right_size)


def complex_product(form, stacked, table_real, table_imag):
    left_side, right_side, result_side = form
    matrix = jnp.stack([jnp.stack([table_real, table_imag]), jnp.stack([-table_imag, table_real])])
    return jnp.einsum(
        "c" + left_side + ",cd" + right_side + "->d" + result_side,
        stacked,
        matrix,
        precision=lax.Precision.HIGHEST,
    )


def complex_times(stacked, other_real, other_imag):
    return jnp.stack(
        [
            stacked[0] * other_real - stacked[1] * other_imag,
            stacked[0] * other_imag + stacked[1] * other_real,
        ]
    )


def forward(stacked, entries, forms):
    left_real, left_imag, right_real, right_imag, twist_real, twist_imag = entries
    stacked = complex_product(forms[0], stacked, left_real, left_imag)
    stacked = complex_times(stacked, twist_real, twist_imag)
    return complex_product(forms[1], stacked, right_real, right_imag)


def split(values):
    high = values.astype(jnp.bfloat16)
    return high, (values - high.astype(jnp.float32)).astype(jnp.bfloat16)


def dot(left, right):
    return jnp.dot(left, right, preferred_element_type=jnp.float32)


def dot_split(left, right):
    return dot(left[0], right[0]) + (dot(left[0], right[1]) + dot(left[1], right[0]))


def chirp_segments(length, taps):
    place = lax.broadcasted_iota(jnp.int32, (taps, 2 * TILE), 1)
    sample = lax.broadcasted_iota(jnp.int32, (taps, 2 * TILE), 0) * TILE - place
    sample = jnp.where(place < TILE, sample, sample + 2 * TILE)
    offset = 2 * sample - length
    numerator = jnp.mod(offset * offset, 8 * length)
    angles = jnp.pi * numerator.astype(jnp.float32) / (4 * length).astype(jnp.float32)
    inside = (sample >= 0) & (sample < length)
    amplitude = jnp.where(inside, 1.0 / jnp.sqrt(length.astype(jnp.float32)), 0.0)
    return jnp.stack([amplitude * jnp.cos(angles), -amplitude * jnp.sin(angles)], axis=1)


def range_kernel(
    taps, shifted, shift_ref, seg_ref, raw_ref, out_ref, real_high, real_low, imag_high, imag_low,
    *rest,
):
    depth = taps * TILE

    @pl.when(pl.program_id(0) == 0)
    def _():
        for tap in range(taps):
            rows = pl.ds(tap * TILE, TILE)
            turned = []
            for part in range(2):
                row = jnp.broadcast_to(seg_ref[tap, pl.ds(part, 1), :], (TILE, 2 * TILE))
                turned.append(pltpu.roll(row, 0, 1, stride=1, stride_axis=0)[:, 0:TILE])
            for part, (columns, high_ref, low_ref) in enumerate(
                (
                    (0, real_high, real_low),
                    (TILE, real_high, real_low),
                )
            ):
                high, low = split(turned[part])
                high_ref[rows, pl.ds(columns, TILE)] = high
                low_ref[rows, pl.ds(columns, TILE)] = low
                if part == 0:
                    imag_high[rows, pl.ds(TILE, TILE)] = high
                    imag_low[rows, pl.ds(TILE, TILE)] = low
                else:
                    imag_high[rows, pl.ds(0, TILE)] = -high
                    imag_low[rows, pl.ds(0, TILE)] = -low
            if shifted:
                edge_real_high, edge_real_low, edge_imag_high, edge_imag_low = rest[1:]
                real, imag = turned[0][:, 0:LANES], turned[1][:, 0:LANES]
                low_half = lax.broadcasted_iota(jnp.int32, (TILE, LANES), 1) < LANES // 2
                high, low = split(jnp.where(low_half, real, pltpu.roll(imag, LANES // 2, 1)))
                edge_real_high[rows], edge_real_low[rows] = high, low
                high, low = split(jnp.where(low_half, -imag, pltpu.roll(real, LANES // 2, 1)))
                edge_imag_high[rows], edge_imag_low[rows] = high, low

    def correlated(start, tabs):
        columns = pl.ds(start, depth)
        real, imag = raw_ref[0, :, columns], raw_ref[1, :, columns]
        return (dot(real, tabs[0][...]) + dot(imag, tabs[2][...])) + (
            dot(real, tabs[1][...]) + dot(imag, tabs[3][...])
        )

    tabs = (real_high, real_low, imag_high, imag_low)
    bins = out_ref.shape[2]
    for block in range(WINDOW // TILE):
        result = correlated(block * TILE, tabs)
        for part in range(2):
            turned = result[:, part * TILE : (part + 1) * TILE].T
            if shifted:
                rest[0][part, pl.ds(MAXSHIFT + block * TILE, TILE), :] = turned
            else:
                out_ref[pl.ds(block * TILE // bins, TILE // bins), part] = turned.reshape(
                    TILE // bins, bins, turned.shape[1]
                )
    if shifted:
        target = rest[0]
        edge = correlated(WINDOW, rest[1:]).T
        for part in range(2):
            target[part, 0:MAXSHIFT, :] = jnp.zeros((MAXSHIFT, edge.shape[1]), jnp.float32)
            target[part, pl.ds(MAXSHIFT + WINDOW, MAXSHIFT), :] = edge[
                part * LANES // 2 : part * LANES // 2 + MAXSHIFT
            ]
        held = WINDOW + 2 * MAXSHIFT
        turn = lax.rem(held - MAXSHIFT + shift_ref[0], held)
        for part in range(2):
            moved = pltpu.roll(target[part], turn, 0)[0:WINDOW]
            out_ref[:, part] = moved.reshape(WINDOW // bins, bins, moved.shape[1])


def range_focus(raw, segments, shift, shifted):
    parts = lax.axis_size("az")
    bins = WINDOW // parts
    taps = segments.shape[0]
    depth = taps * TILE
    lines_count = raw.shape[1]
    height = min(TILE, lines_count)
    width = depth + WINDOW
    scratch = [pltpu.VMEM((depth, 2 * TILE), jnp.bfloat16)] * 4
    if shifted:
        scratch += [pltpu.VMEM((2, WINDOW + 2 * MAXSHIFT, height), jnp.float32)]
        scratch += [pltpu.VMEM((depth, LANES), jnp.bfloat16)] * 4
    return pl.pallas_call(
        functools.partial(range_kernel, taps, shifted),
        out_shape=jax.ShapeDtypeStruct((parts, 2, bins, lines_count), jnp.float32),
        grid=(lines_count // height,),
        in_specs=[
            pl.BlockSpec(memory_space=pltpu.SMEM),
            pl.BlockSpec((taps, 2, 2 * TILE), lambda i: (0, 0, 0)),
            pl.BlockSpec((2, height, width), lambda i: (0, i, 0)),
        ],
        out_specs=pl.BlockSpec((parts, 2, bins, height), lambda i: (0, 0, 0, i)),
        scratch_shapes=scratch,
        compiler_params=pltpu.CompilerParams(vmem_limit_bytes=VMEM_BYTES),
        cost_estimate=pl.CostEstimate(
            flops=16 * lines_count * depth * WINDOW,
            bytes_accessed=4 * lines_count * (width + 2 * WINDOW),
            transcendentals=0,
        ),
        name="range_second" if shifted else "range_first",
    )(shift, segments, raw)


def azimuth_image(in_ref, spec_ref, left_ref, right_ref, twist_ref):
    parts, _, bins, lines_count = in_ref.shape
    lines = parts * lines_count
    left_size = lines // LANES
    real, imag = (
        jnp.concatenate([in_ref[one, part] for one in range(parts)], axis=1).reshape(
            bins, left_size, LANES
        )
        for part in range(2)
    )
    twist_real, twist_imag = twist_ref[0], twist_ref[1]
    middle_real, middle_imag = [], []
    for one in range(0, bins, 2):
        pair = jnp.concatenate(
            [
                jnp.concatenate([real[one], imag[one]], axis=0),
                jnp.concatenate([real[one + 1], imag[one + 1]], axis=0),
            ],
            axis=1,
        )
        turned = dot_split((left_ref[0], left_ref[1]), split(pair))
        for half in range(2):
            columns = slice(half * LANES, (half + 1) * LANES)
            upper, lower = turned[0:left_size, columns], turned[left_size:, columns]
            middle_real.append(upper * twist_real - lower * twist_imag)
            middle_imag.append(upper * twist_imag + lower * twist_real)
    stacked = jnp.concatenate(
        [jnp.concatenate(middle_real, axis=0), jnp.concatenate(middle_imag, axis=0)], axis=1
    )
    spectrum = dot_split(split(stacked), (right_ref[0], right_ref[1]))
    upper = spectrum[:, 0:LANES].reshape(bins, left_size, LANES)
    lower = spectrum[:, LANES:].reshape(bins, left_size, LANES)
    spec_real, spec_imag = spec_ref[0][None], spec_ref[1][None]
    stacked = jnp.concatenate(
        [
            (upper * spec_real - lower * spec_imag).reshape(bins * left_size, LANES),
            (upper * spec_imag + lower * spec_real).reshape(bins * left_size, LANES),
        ],
        axis=1,
    )
    stacked = dot_split(split(stacked), (right_ref[2], right_ref[3]))
    upper = stacked[:, 0:LANES].reshape(bins, left_size, LANES)
    lower = stacked[:, LANES:].reshape(bins, left_size, LANES)
    middle_real = upper * twist_real[None] + lower * twist_imag[None]
    middle_imag = lower * twist_real[None] - upper * twist_imag[None]
    result_real, result_imag = [], []
    for one in range(0, bins, 2):
        pair = jnp.concatenate(
            [
                jnp.concatenate([middle_real[one], middle_imag[one]], axis=0),
                jnp.concatenate([middle_real[one + 1], middle_imag[one + 1]], axis=0),
            ],
            axis=1,
        )
        turned = dot_split((left_ref[2], left_ref[3]), split(pair))
        for half in range(2):
            columns = slice(half * LANES, (half + 1) * LANES)
            result_real.append(turned[0:left_size, columns])
            result_imag.append(turned[left_size:, columns])
    return (
        jnp.stack(result_real).reshape(bins, lines),
        jnp.stack(result_imag).reshape(bins, lines),
    )


def first_kernel(in_ref, spec_ref, left_ref, right_ref, twist_ref, out_ref):
    out_ref[0], out_ref[1] = azimuth_image(in_ref, spec_ref, left_ref, right_ref, twist_ref)


def azimuth_box(values):
    rows, lines = values.shape
    values = jnp.concatenate([values, jnp.zeros((rows, LANES), jnp.float32)], axis=1)
    total = lines + LANES
    for step in (1, 2, 4):
        values = values + pltpu.roll(values, total - step, 1)
    return pltpu.roll(values, 3, 1)[:, 0:lines]


def second_kernel(
    shift_ref, in_ref, first_ref, spec_ref, left_ref, right_ref, twist_ref, out_ref
):
    real, imag = azimuth_image(in_ref, spec_ref, left_ref, right_ref, twist_ref)
    source = lax.broadcasted_iota(jnp.int32, real.shape, 1) - shift_ref[0]
    inside = (source >= 0) & (source < real.shape[1])
    real, imag = jnp.where(inside, real, 0.0), jnp.where(inside, imag, 0.0)
    first_real, first_imag = first_ref[0], first_ref[1]
    out_ref[0] = azimuth_box(first_real * real + first_imag * imag)
    out_ref[1] = azimuth_box(first_imag * real - first_real * imag)
    out_ref[2] = azimuth_box(first_real * first_real + first_imag * first_imag)
    out_ref[3] = azimuth_box(real * real + imag * imag)


def azimuth_call(ranged, spec, tabs, first=None, shift=None):
    left, right, twist = tabs
    parts, _, bins, lines_count = ranged.shape
    lines = parts * lines_count
    height = 8

    def whole(array):
        return pl.BlockSpec(array.shape, lambda i: (0,) * array.ndim)

    block = pl.BlockSpec((2, height, lines), lambda i: (0, i, 0))
    source = pl.BlockSpec((parts, 2, height, lines_count), lambda i: (0, 0, i, 0))
    operands, specs = [ranged], [source]
    if first is not None:
        operands = [shift, ranged, first]
        specs = [pl.BlockSpec(memory_space=pltpu.SMEM), source, block]
    constants = [spec, left, right, twist]
    outs = 2 if first is None else 4
    return pl.pallas_call(
        first_kernel if first is None else second_kernel,
        out_shape=jax.ShapeDtypeStruct((outs, bins, lines), jnp.float32),
        grid=(bins // height,),
        in_specs=specs + [whole(array) for array in constants],
        out_specs=pl.BlockSpec((outs, height, lines), lambda i: (0, i, 0)),
        compiler_params=pltpu.CompilerParams(vmem_limit_bytes=VMEM_BYTES),
        cost_estimate=pl.CostEstimate(
            flops=24 * 512 * bins * lines,
            bytes_accessed=4 * bins * lines * (2 + outs),
            transcendentals=0,
        ),
        name="azimuth_first" if first is None else "azimuth_second",
    )(*operands, *constants)


def range_box_kernel(sums_ref, low_ref, high_ref, inter_ref, coherence_ref, scratch):
    bins = sums_ref.shape[1]
    boxes = []
    for part in range(4):
        scratch[4:8, :] = low_ref[part]
        scratch[pl.ds(8, bins), :] = sums_ref[part]
        scratch[pl.ds(8 + bins, 4), :] = high_ref[part]
        values = scratch[pl.ds(5, bins + 7), :]
        values = values[:-1] + values[1:]
        values = values[:-2] + values[2:]
        boxes.append(values[:-4] + values[4:])
    inter_ref[0] = boxes[0] * (1.0 / 64.0)
    inter_ref[1] = boxes[1] * (1.0 / 64.0)
    coherence_ref[...] = jnp.sqrt(boxes[0] * boxes[0] + boxes[1] * boxes[1]) / jnp.sqrt(
        boxes[2] * boxes[3] + 1.0
    )


def range_box(sums, low, high):
    _, bins, lines = sums.shape
    width = 512
    return pl.pallas_call(
        range_box_kernel,
        out_shape=(
            jax.ShapeDtypeStruct((2, bins, lines), jnp.float32),
            jax.ShapeDtypeStruct((bins, lines), jnp.float32),
        ),
        grid=(lines // width,),
        in_specs=[
            pl.BlockSpec((4, bins, width), lambda i: (0, 0, i)),
            pl.BlockSpec((4, 4, width), lambda i: (0, 0, i)),
            pl.BlockSpec((4, 4, width), lambda i: (0, 0, i)),
        ],
        out_specs=(
            pl.BlockSpec((2, bins, width), lambda i: (0, 0, i)),
            pl.BlockSpec((bins, width), lambda i: (0, i)),
        ),
        scratch_shapes=[pltpu.VMEM((bins + 16, width), jnp.float32)],
        compiler_params=pltpu.CompilerParams(vmem_limit_bytes=VMEM_BYTES),
        name="range_box",
    )(sums, low, high)


def stacked_tables(real, imag, left):
    if left:
        real_form = jnp.concatenate(
            [jnp.concatenate([real, -imag], 1), jnp.concatenate([imag, real], 1)], 0
        )
    else:
        real_form = jnp.concatenate(
            [jnp.concatenate([real, imag], 1), jnp.concatenate([-imag, real], 1)], 0
        )
    high = lax.reduce_precision(real_form, 8, 7)
    return high.astype(jnp.bfloat16), (real_form - high).astype(jnp.bfloat16)


def neighbours(block, axis, width):
    count = lax.axis_size(axis)
    ahead = [(i, i + 1) for i in range(count - 1)]
    back = [(target, source) for source, target in ahead]
    return (
        lax.ppermute(block[:, -width:], axis, ahead),
        lax.ppermute(block[:, :width], axis, back),
    )


def on_device(raw_first, raw_second, offsets, chirp_lengths):
    lines_count = raw_first.shape[1]
    range_count = raw_first.shape[2]
    azimuth_count = lines_count * lax.axis_size("az")
    longest = min(range_count, azimuth_count) // 4
    segments = chirp_segments(chirp_lengths[0], longest // TILE + 1)
    first_ranged = range_focus(raw_first, segments, offsets[1:2], False)
    second_ranged = range_focus(raw_second, segments, offsets[1:2], True)
    first_turned = lax.all_to_all(first_ranged, "az", split_axis=0, concat_axis=0, tiled=True)
    second_turned = lax.all_to_all(second_ranged, "az", split_axis=0, concat_axis=0, tiled=True)

    entries, left_size, right_size = tables(azimuth_count)
    left_real, left_imag, right_real, right_imag, twist_real, twist_imag = entries
    left = jnp.stack(
        stacked_tables(left_real, left_imag, True) + stacked_tables(left_real, -left_imag, True)
    )
    right = jnp.stack(
        stacked_tables(right_real, right_imag, False)
        + stacked_tables(right_real, -right_imag, False)
    )
    tabs = (left, right, jnp.stack([twist_real, twist_imag]))
    chirp_real, chirp_imag = chirp(chirp_lengths[1], azimuth_count)
    spec = forward(
        jnp.stack([chirp_real, chirp_imag]).reshape(2, 1, left_size, right_size),
        entries,
        along_forms,
    )[:, 0]
    spec = jnp.stack([spec[0], -spec[1]]) * (1.0 / azimuth_count)
    frequency = lax.broadcasted_iota(
        jnp.int32, (left_size, right_size), 0
    ) + left_size * lax.broadcasted_iota(jnp.int32, (left_size, right_size), 1)
    turns = jnp.mod(frequency * offsets[0], azimuth_count).astype(jnp.float32)
    angles = -2.0 * math.pi / azimuth_count * turns
    second_spec = complex_times(spec, jnp.cos(angles), jnp.sin(angles))

    first_image = azimuth_call(first_turned, spec, tabs)
    sums = azimuth_call(second_turned, second_spec, tabs, first_image, offsets[0:1])
    low, high = neighbours(sums, "az", 4)
    return range_box(sums, low, high)


def solution(mesh):
    in_specs = (P("groups", "az", None), P("groups", "az", None), P("groups"), P("groups"))
    out_specs = (P("groups", "az", None), P(("groups", "az"), None))
    return jax.shard_map(
        on_device, mesh=mesh, in_specs=in_specs, out_specs=out_specs, check_vma=False
    )
```

profile of v0, /device:TPU:15, one launch (start us, length us, event | category | flops | bytes accessed | tf_op | source)
XLA Modules:
  0.0 282.1 jit_solution(10340764260956505234)
XLA Ops:
  0.7 1.4 fusion.80
  2.0 1.3 fusion.79
  5.3 2.8 cosine_multiply_fusion
  8.1 0.7 pad_maximum_fusion.12.seg_ref
  8.8 25.4 %range_first.1 = f32[16,2,64,512]{3,2,1,0:T(8,128)} custom-call(s32[1]{0:T(128)} %get-tuple-element.38.shift_ref, f32[9,2,512]{2,1,0:T(2,128)} %pad_maximum_fusion.12.seg_ref, bf16[2,512,8192]{2,1,0:T(8,128)(2,1)} %raw_ref.3), custom_call_target="tpu_custom_call" | custom-call | flops 19327352832 | bytes 11010048 | tf_op jit(solution)/shard_map/range_first/pallas_call | solution.py:204
  34.2 6.5 %all-to-all-start.1 = ((f32[16,2,64,512]{3,2,1,0:T(8,128)}), f32[16,2,64,512]{3,2,1,0:T(8,128)}, u32[]{:S(2)}, u32[]{:S(2)}) async-start(f32[16,2,64,512]{3,2,1,0:T(8,128)} %range_first.1), calls=%async_computation.1 | async-start | bytes 8388608 | tf_op jit(solution)/shard_map/all_to_all | solution.py:424
  40.7 29.4 %range_second.1 = f32[16,2,64,512]{3,2,1,0:T(8,128)} custom-call(s32[1]{0:T(128)} %get-tuple-element.38.shift_ref, f32[9,2,512]{2,1,0:T(2,128)} %pad_maximum_fusion.12.seg_ref, bf16[2,512,8192]{2,1,0:T(8,128)(2,1)} %raw_ref.2), custom_call_target="tpu_custom_call" | custom-call | flops 19327352832 | bytes 11010048 | tf_op jit(solution)/shard_map/range_second/pallas_call | solution.py:204
  70.1 63.1 %all-to-all-done.1.in_ref = f32[16,2,64,512]{3,2,1,0:T(8,128)} async-done(((f32[16,2,64,512]{3,2,1,0:T(8,128)}), f32[16,2,64,512]{3,2,1,0:T(8,128)}, u32[]{:S(2)}, u32[]{:S(2)}) %all-to-all-start.1) | async-done | bytes 4194336 | tf_op jit(solution)/shard_map/all_to_all | solution.py:424
  133.1 4.8 %all-to-all-start = ((f32[16,2,64,512]{3,2,1,0:T(8,128)}), f32[16,2,64,512]{3,2,1,0:T(8,128)}, u32[]{:S(2)}, u32[]{:S(2)}) async-start(f32[16,2,64,512]{3,2,1,0:T(8,128)} %range_second.1), calls=%async_computation | async-start | bytes 8388608 | tf_op jit(solution)/shard_map/all_to_all | solution.py:425
  139.7 0.1 fusion.74
  139.8 0.1 fusion.72
  139.9 1.1 select_multiply_fusion
  141.0 0.3 convolution_bitcast_fusion.1
  141.3 0.1 fusion.75
  141.5 0.1 fusion.69
  141.6 0.1 fusion.68
  141.8 0.3 fusion.65
  142.0 0.3 fusion.64
  142.3 0.3 fusion.47
  142.6 0.3 fusion.46
  142.8 0.1 fusion.70
  143.0 0.6 pad_maximum_fusion.10.twist_ref
  143.6 0.3 fusion.57
  143.9 0.2 subtract_bitcast_fusion
  144.1 0.3 convolution_bitcast_fusion
  144.4 0.0 copy-start.2
  144.4 0.7 multiply_subtract_fusion
  145.1 0.6 pad_maximum_fusion.11.spec_ref
  145.7 0.1 maximum_bitcast_fusion.8
  145.9 0.7 pad_maximum_fusion.7.left_ref
  146.6 0.1 reduce-precision_convert_fusion
  146.7 0.9 pad_maximum_fusion.right_ref
  147.5 0.0 copy-done.2
  147.5 14.8 %azimuth_first.1.first_ref = f32[2,64,8192]{2,1,0:T(8,128)} custom-call(f32[16,2,64,512]{3,2,1,0:T(8,128)} %all-to-all-done.1.in_ref, f32[2,64,128]{2,1,0:T(8,128)} %copy-done.2, bf16[4,128,128]{2,1,0:T(8,128)(2,1)} %pad_maximum_fusion.7.left_ref, bf16[4,256,256]{2,1,0:T(8,128)(2,1)} %pad_maximum_fusion.right_ref, f32[2,64,128]{2,1,0:T(8,128)} %pad_maximum_fusion.10.twist_ref), custom_call_target="tpu_custom_call" | custom-call | flops 6442450944 | bytes 8388608 | tf_op jit(solution)/shard_map/azimuth_first/pallas_call | solution.py:334
  162.3 68.1 %all-to-all-done.in_ref = f32[16,2,64,512]{3,2,1,0:T(8,128)} async-done(((f32[16,2,64,512]{3,2,1,0:T(8,128)}), f32[16,2,64,512]{3,2,1,0:T(8,128)}, u32[]{:S(2)}, u32[]{:S(2)}) %all-to-all-start) | async-done | bytes 4194336 | tf_op jit(solution)/shard_map/all_to_all | solution.py:425
  230.4 22.9 %azimuth_second.1.sums_ref = f32[4,64,8192]{2,1,0:T(8,128)} custom-call(s32[1]{0:T(128)} %get-tuple-element.39.shift_ref, f32[16,2,64,512]{3,2,1,0:T(8,128)} %all-to-all-done.in_ref, f32[2,64,8192]{2,1,0:T(8,128)} %azimuth_first.1.first_ref, f32[2,64,128]{2,1,0:T(8,128)} %pad_maximum_fusion.11.spec_ref, bf16[4,128,128]{2,1,0:T(8,128)(2,1)} %pad_maximum_fusion.7.left_ref, ...), custom_call_target="tpu_custom_call" | custom-call | flops 6442450944 | bytes 12582912 | tf_op jit(solution)/shard_map/azimuth_second/pallas_call | solution.py:334
  253.3 1.7 fusion.78
  255.0 2.0 collective-permute-start.1
  257.0 4.4 %collective-permute-start = (f32[4,4,8192]{2,1,0:T(4,128)S(1)}, f32[4,4,8192]{2,1,0:T(4,128)S(1)}, u32[]{:S(2)}, u32[]{:S(2)}) collective-permute-start(f32[4,4,8192]{2,1,0:T(4,128)S(1)} %get-tuple-element.3), channel_id=1, source_target_pairs={{0,1},{1,2},{2,3},{3,4},{4,5},{5,6},{6,7},{7,8},{8,9},{9,10},{10,1... | collective-permute-start | bytes 1572872 | tf_op jit(solution)/shard_map/ppermute | solution.py:411
  261.5 5.0 %collective-permute-done.1.high_ref = f32[4,4,8192]{2,1,0:T(4,128)S(1)} collective-permute-done((f32[4,4,8192]{2,1,0:T(4,128)S(1)}, f32[4,4,8192]{2,1,0:T(4,128)S(1)}, u32[]{:S(2)}, u32[]{:S(2)}) %collective-permute-start.1) | collective-permute-done | bytes 524320 | tf_op jit(solution)/shard_map/ppermute | solution.py:412
  266.5 0.0 copy-start
  266.5 1.1 collective-permute-done.low_ref
  267.6 0.0 copy-done
  267.6 0.0 copy-start.1
  267.6 0.9 copy-done.1
  268.5 13.6 %range_box.1 = (f32[2,64,8192]{2,1,0:T(8,128)}, f32[64,8192]{1,0:T(8,128)}) custom-call(f32[4,64,8192]{2,1,0:T(8,128)} %azimuth_second.1.sums_ref, f32[4,4,8192]{2,1,0:T(4,128)} %copy-done.1, f32[4,4,8192]{2,1,0:T(4,128)} %copy-done), custom_call_target="tpu_custom_call" | custom-call | tf_op jit(solution)/shard_map/range_box/pallas_call | solution.py:371
  (9 shorter events, 0.1 us)
Async XLA Ops:
  34.2 99.0 %all-to-all-start.1 = ((f32[16,2,64,512]{3,2,1,0:T(8,128)}), f32[16,2,64,512]{3,2,1,0:T(8,128)}, u32[]{:S(2)}, u32[]{:S(2)}) async-start(f32[16,2,64,512]{3,2,1,0:T(8,128)} %range_first.1), calls=%async_computation.1 | async-start | bytes 8388608 | tf_op jit(solution)/shard_map/all_to_all | solution.py:424
  133.1 97.2 %all-to-all-start = ((f32[16,2,64,512]{3,2,1,0:T(8,128)}), f32[16,2,64,512]{3,2,1,0:T(8,128)}, u32[]{:S(2)}, u32[]{:S(2)}) async-start(f32[16,2,64,512]{3,2,1,0:T(8,128)} %range_second.1), calls=%async_computation | async-start | bytes 8388608 | tf_op jit(solution)/shard_map/all_to_all | solution.py:425
  144.4 3.2 %copy-start.2 = (f32[2,64,128]{2,1,0:T(8,128)}, f32[2,64,128]{2,1,0:T(8,128)S(1)}, u32[]{:S(2)}) copy-start(f32[2,64,128]{2,1,0:T(8,128)S(1)} %maximum_multiply_fusion.spec_ref) | copy-start | bytes 196612
  255.0 11.5 %collective-permute-start.1 = (f32[4,4,8192]{2,1,0:T(4,128)S(1)}, f32[4,4,8192]{2,1,0:T(4,128)S(1)}, u32[]{:S(2)}, u32[]{:S(2)}) collective-permute-start(f32[4,4,8192]{2,1,0:T(4,128)S(1)} %get-tuple-element.2), channel_id=1, source_target_pairs={{1,0},{2,1},{3,2},{4,3},{5,4},{6,5},{7,6},{8,7},{9,8},{10,9},{11,1... | collective-permute-start | bytes 1572872 | tf_op jit(solution)/shard_map/ppermute | solution.py:412
  257.0 10.6 %collective-permute-start = (f32[4,4,8192]{2,1,0:T(4,128)S(1)}, f32[4,4,8192]{2,1,0:T(4,128)S(1)}, u32[]{:S(2)}, u32[]{:S(2)}) collective-permute-start(f32[4,4,8192]{2,1,0:T(4,128)S(1)} %get-tuple-element.3), channel_id=1, source_target_pairs={{0,1},{1,2},{2,3},{3,4},{4,5},{5,6},{6,7},{7,8},{8,9},{9,10},{10,1... | collective-permute-start | bytes 1572872 | tf_op jit(solution)/shard_map/ppermute | solution.py:411
  266.5 1.1 copy-start
  267.6 0.9 copy-start.1
where the time goes:
time: 287 us; the launch traced here: 282 us
  waiting for transfers between devices  137 us (48%)
  Pallas kernels  106 us (37%)
  starting transfers between devices  17.8 us (6%)
  other arithmetic  10.6 us (4%)
  local copies, waits for them, and re-layouts  5.27 us (2%)
  between operations  4.53 us (2%)
    all_to_all x1, waiting for transfers between devices, on_device(): lax.all_to_all(second_ranged, 'az', split_axis=0, concat_axis=0, tiled=True)  68.1 us
    all_to_all x1, waiting for transfers between devices, on_device(): lax.all_to_all(first_ranged, 'az', split_axis=0, concat_axis=0, tiled=True)  63.1 us
    pallas_call x2, Pallas kernels, range_focus(): pl.pallas_call(functools.partial(range_kernel, taps, shifted), out_shape=...  54.8 us
    pallas_call x2, Pallas kernels, azimuth_call(): pl.pallas_call(first_kernel if first is None else second_kernel, out_shap...  37.7 us
    pallas_call x1, Pallas kernels, range_box(): pl.pallas_call(range_box_kernel, out_shape=(jax.ShapeDtypeStruct((2, bins...  13.6 us
    all_to_all x1, starting transfers between devices, on_device(): lax.all_to_all(first_ranged, 'az', split_axis=0, concat_axis=0, tiled=True)  6.52 us
  transfers between devices with their start and end apart: 4, of which 4 were waited for; matrix products, arithmetic and copies ran while one was open for 3% of the time, Pallas kernels for 16%

commit v1 on v0

--- a/solution.py
+++ b/solution.py
@@ -3,6 +3,7 @@
 
 import jax
 import jax.numpy as jnp
+import numpy as np
 from jax import lax
 from jax.experimental import pallas as pl
 from jax.experimental.pallas import tpu as pltpu
@@ -413,7 +414,7 @@
     )
 
 
-def on_device(raw_first, raw_second, offsets, chirp_lengths):
+def staged_on_device(raw_first, raw_second, offsets, chirp_lengths):
     lines_count = raw_first.shape[1]
     range_count = raw_first.shape[2]
     azimuth_count = lines_count * lax.axis_size("az")
@@ -454,6 +455,459 @@
     return range_box(sums, low, high)
 
 
+ROWS = 8
+
+
+def host_tables(lines):
+    left_size, right_size = lines // LANES, LANES
+
+    def turn(rows_count, cols_count, period):
+        product = np.outer(np.arange(rows_count), np.arange(cols_count)) % period
+        angles = -2.0 * np.pi / period * product
+        return np.cos(angles), np.sin(angles)
+
+    def stacked(real, imag, left):
+        sign = -1.0 if left else 1.0
+        form = np.block([[real, sign * imag], [-sign * imag, real]]).astype(np.float32)
+        high = form.astype(jnp.bfloat16)
+        low = (form - high.astype(np.float32)).astype(jnp.bfloat16)
+        return [high, low]
+
+    left_real, left_imag = turn(left_size, left_size, left_size)
+    right_real, right_imag = turn(right_size, right_size, right_size)
+    twist = turn(left_size, right_size, lines)
+    left = np.stack(stacked(left_real, left_imag, True) + stacked(left_real, -left_imag, True))
+    right = np.stack(
+        stacked(right_real, right_imag, False) + stacked(right_real, -right_imag, False)
+    )
+    return jnp.asarray(left), jnp.asarray(right), jnp.asarray(np.stack(twist).astype(np.float32))
+
+
+def chirp_values(sample, length):
+    inside = (sample >= 0) & (sample < length)
+    offset = 2 * jnp.clip(sample, 0, length) - length
+    period = 8 * length
+    square = offset * offset
+    turns = jnp.floor(square.astype(jnp.float32) / period.astype(jnp.float32)).astype(jnp.int32)
+    numerator = square - turns * period
+    numerator = jnp.where(numerator < 0, numerator + period, numerator)
+    numerator = jnp.where(numerator >= period, numerator - period, numerator)
+    scale = length.astype(jnp.float32)
+    angles = jnp.pi * numerator.astype(jnp.float32) / (4.0 * scale)
+    amplitude = jnp.where(inside, 1.0 / jnp.sqrt(jnp.full(sample.shape, scale)), 0.0)
+    return amplitude * jnp.cos(angles), amplitude * jnp.sin(angles)
+
+
+def azimuth_filter(length, shift, lines, left_ref, right_ref, twist_ref, spec_ref):
+    left_size = lines // LANES
+    shape = (left_size, LANES)
+    row, column = (lax.broadcasted_iota(jnp.int32, shape, axis) for axis in range(2))
+    real, imag = chirp_values(row * LANES + column, length)
+    turned = dot_split(
+        (left_ref[0], left_ref[1]), split(jnp.concatenate([real, imag], axis=0))
+    )
+    upper, lower = turned[0:left_size], turned[left_size:]
+    twist_real, twist_imag = twist_ref[0], twist_ref[1]
+    stacked = jnp.concatenate(
+        [upper * twist_real - lower * twist_imag, upper * twist_imag + lower * twist_real], axis=1
+    )
+    stacked = dot_split(split(stacked), (right_ref[0], right_ref[1])) * (1.0 / lines)
+    real, imag = stacked[:, 0:LANES], -stacked[:, LANES:]
+    spec_ref[0, 0], spec_ref[0, 1] = real, imag
+    frequency = row + left_size * column
+    turns = ((frequency * shift) & (lines - 1)).astype(jnp.float32)
+    angles = (-2.0 * math.pi / lines) * turns
+    turn_real, turn_imag = jnp.cos(angles), jnp.sin(angles)
+    spec_ref[1, 0] = real * turn_real - imag * turn_imag
+    spec_ref[1, 1] = real * turn_imag + imag * turn_real
+
+
+def build_table(taps, lead, length, seg_ref, tab_ref):
+    rows = seg_ref.shape[1]
+    place = lax.broadcasted_iota(jnp.int32, (rows, 2 * TILE), 1)
+    sample = lax.broadcasted_iota(jnp.int32, (rows, 2 * TILE), 0) * TILE - place
+    sample = jnp.where(place < TILE, sample, sample + 2 * TILE) + lead
+    real, imag = chirp_values(sample, length)
+    seg_ref[0], seg_ref[1] = real, -imag
+
+    def one(tap, carry):
+        rows = pl.ds(pl.multiple_of(tap * TILE, TILE), TILE)
+        for part in range(2):
+            row = jnp.broadcast_to(seg_ref[part, pl.ds(tap, 1), :], (TILE, 2 * TILE))
+            turned = pltpu.roll(row, 0, 1, stride=1, stride_axis=0)[:, 0:TILE]
+            high, low = split(turned)
+            columns, other = pl.ds(part * TILE, TILE), pl.ds((1 - part) * TILE, TILE)
+            tab_ref[0, rows, columns] = high
+            tab_ref[1, rows, columns] = low
+            tab_ref[2, rows, other] = high if part == 0 else -high
+            tab_ref[3, rows, other] = low if part == 0 else -low
+        return carry
+
+    lax.fori_loop(0, taps, one, 0)
+
+
+def fused_kernel(
+    parts, taps,
+    offset_ref, length_ref, raw_first, raw_second, left_ref, right_ref, twist_ref,
+    inter_ref, coherence_ref,
+    raw, tab, seg, spec, sent_first, sent_second, got_first, got_second, image, sums,
+    edge_sent, edge_got, inter_out, coherence_out,
+    raw_sem, first_send, first_recv, second_send, second_recv, edge_send_sem, edge_recv_sem,
+    out_sem,
+):
+    me = lax.axis_index("az")
+    bins, lines_count = sent_first.shape[2], sent_first.shape[3]
+    lines = parts * lines_count
+    groups = bins // ROWS
+    halves = lines_count // TILE
+    blocks = WINDOW // TILE
+    per_block = TILE // bins
+    last = parts - 1
+
+    def load(source):
+        width = raw.shape[2] - LANES
+        return pltpu.make_async_copy(
+            source.at[:, :, pl.ds(0, width)], raw.at[:, :, pl.ds(LANES, width)], raw_sem.at[0]
+        )
+
+    load(raw_first).start()
+    barrier = pltpu.get_barrier_semaphore()
+
+    def greet(step, carry):
+        pl.semaphore_signal(barrier, inc=1, device_id={"az": lax.rem(me + step, parts)})
+        return carry
+
+    lax.fori_loop(1, parts, greet, 0)
+    raw[:, :, 0:LANES] = jnp.zeros((2, lines_count, LANES), jnp.bfloat16)
+    build_table(taps, 0, length_ref[0], seg, tab)
+    load(raw_first).wait()
+    pl.semaphore_wait(barrier, parts - 1)
+
+    half = me // (parts // 2)
+    turn = lax.rem(me // per_block, blocks // 2)
+
+    def block_of(step):
+        side = lax.rem(half + 1 + step // (blocks // 2), 2)
+        return side * (blocks // 2) + lax.rem(step + turn, blocks // 2)
+
+    def correlate(block, piece, start, depth, target, low):
+        rows = pl.ds(pl.multiple_of(piece * TILE, TILE), TILE)
+        columns = pl.ds(pl.multiple_of(start + block * TILE, LANES), depth)
+        real, imag = raw[0, rows, columns], raw[1, rows, columns]
+        table = pl.ds(0, depth)
+        result = (dot(real, tab[0, table]) + dot(imag, tab[2, table])) + (
+            dot(real, tab[1, table]) + dot(imag, tab[3, table])
+        )
+        for part in range(2):
+            turned = result[:, part * TILE : (part + 1) * TILE].T
+            if low is not None:
+                place = block * TILE + lax.broadcasted_iota(jnp.int32, (TILE, TILE), 0)
+                turned = jnp.where(place >= low, turned, 0.0)
+            turned = turned.reshape(per_block, bins, TILE)
+            where = pl.ds(block * per_block, per_block)
+            target[where, part, ROWS:bins, rows] = turned[:, 0 : bins - ROWS]
+            target[where, part, 0:ROWS, rows] = turned[:, bins - ROWS : bins]
+
+    def first_copy(piece, dest, source):
+        rows = pl.ds(pl.multiple_of(piece * TILE, TILE), TILE)
+        return pltpu.make_async_remote_copy(
+            src_ref=sent_first.at[dest, :, :, rows],
+            dst_ref=got_first.at[source, :, :, rows],
+            send_sem=first_send.at[piece, dest],
+            recv_sem=first_recv.at[piece, source],
+            device_id={"az": dest},
+        )
+
+    def first_tile(step, carry):
+        block, piece = block_of(step // halves), lax.rem(step, halves)
+        correlate(block, piece, LANES, taps * TILE, sent_first, None)
+
+        def send(item, inner):
+            dest = block * per_block + lax.rem(item + me, per_block)
+
+            @pl.when(dest != me)
+            def _():
+                first_copy(piece, dest, me).start()
+
+            return inner
+
+        lax.fori_loop(0, per_block, send, 0)
+        return carry
+
+    lax.fori_loop(0, blocks * halves, first_tile, 0)
+
+    load(raw_second).start()
+    build_table(taps + 1, offset_ref[1] - LANES, length_ref[0], seg, tab)
+    load(raw_second).wait()
+
+    def second_tile(step, carry):
+        correlate(
+            step // halves, lax.rem(step, halves), 0, (taps + 1) * TILE, sent_second,
+            offset_ref[1],
+        )
+        return carry
+
+    lax.fori_loop(0, blocks * halves, second_tile, 0)
+
+    def second_copy(group, dest, source):
+        rows = pl.ds(pl.multiple_of(group * ROWS, ROWS), ROWS)
+        return pltpu.make_async_remote_copy(
+            src_ref=sent_second.at[dest, :, rows, :],
+            dst_ref=got_second.at[source, :, rows, :],
+            send_sem=second_send.at[group, dest],
+            recv_sem=second_recv.at[group, source],
+            device_id={"az": dest},
+        )
+
+    def send_second(start, stop):
+        def send(item, carry):
+            group, step = start + item // last, 1 + lax.rem(item, last)
+            second_copy(group, lax.rem(me + step, parts), me).start()
+            return carry
+
+        lax.fori_loop(0, (stop - start) * last, send, 0)
+
+    early = groups // 2
+    send_second(0, early)
+    got_first[me] = sent_first[me]
+    got_second[me] = sent_second[me]
+    sums[:, 0:ROWS, :] = jnp.zeros((4, ROWS, lines), jnp.float32)
+    sums[:, pl.ds(ROWS + bins, ROWS), :] = jnp.zeros((4, ROWS, lines), jnp.float32)
+    azimuth_filter(length_ref[1], offset_ref[0], lines, left_ref, right_ref, twist_ref, spec)
+
+    def first_arrived(item, carry):
+        piece, source = item // last, lax.rem(me + 1 + lax.rem(item, last), parts)
+        first_copy(piece, source, source).wait_recv()
+        return carry
+
+    lax.fori_loop(0, halves * last, first_arrived, 0)
+
+    def first_group(group, carry):
+        rows = pl.ds(pl.multiple_of(group * ROWS, ROWS), ROWS)
+        real, imag = azimuth_image(
+            got_first.at[:, :, rows, :], spec.at[0], left_ref, right_ref, twist_ref
+        )
+        image[0, rows, :] = real
+        image[1, rows, :] = imag
+        return carry
+
+    lax.fori_loop(0, groups, first_group, 0)
+
+    def edge_copy(side, dest):
+        return pltpu.make_async_remote_copy(
+            src_ref=edge_sent.at[side],
+            dst_ref=edge_got.at[side],
+            send_sem=edge_send_sem.at[side],
+            recv_sem=edge_recv_sem.at[side],
+            device_id={"az": dest},
+        )
+
+    def out_copies(group):
+        rows = pl.ds(pl.multiple_of(group * ROWS, ROWS), ROWS)
+        return (
+            pltpu.make_async_copy(
+                inter_out.at[:, rows, :], inter_ref.at[:, rows, :], out_sem.at[0, group]
+            ),
+            pltpu.make_async_copy(
+                coherence_out.at[rows, :], coherence_ref.at[rows, :], out_sem.at[1, group]
+            ),
+        )
+
+    width = 4 * LANES
+
+    def finish(group):
+        start = group * ROWS
+
+        def piece(item, carry):
+            columns = pl.ds(pl.multiple_of(item * width, width), width)
+            boxes = []
+            for part in range(4):
+                held = sums[part, pl.ds(pl.multiple_of(start, ROWS), 3 * ROWS), columns]
+                for step in (1, 2, 4):
+                    held = held + pltpu.roll(held, 3 * ROWS - step, 0)
+                boxes.append(pltpu.roll(held, 3 * ROWS - 5, 0)[0:ROWS])
+            rows = pl.ds(pl.multiple_of(start, ROWS), ROWS)
+            inter_out[0, rows, columns] = boxes[0] * (1.0 / 64.0)
+            inter_out[1, rows, columns] = boxes[1] * (1.0 / 64.0)
+            coherence_out[rows, columns] = jnp.sqrt(
+                boxes[0] * boxes[0] + boxes[1] * boxes[1]
+            ) / jnp.sqrt(boxes[2] * boxes[3] + 1.0)
+            return carry
+
+        lax.fori_loop(0, lines // width, piece, 0)
+        for copy in out_copies(group):
+            copy.start()
+
+    def second_group(group, carry):
+        def arrived(step, inner):
+            source = lax.rem(me + step, parts)
+            second_copy(group, source, source).wait_recv()
+            return inner
+
+        lax.fori_loop(1, parts, arrived, 0)
+        rows = pl.ds(pl.multiple_of(group * ROWS, ROWS), ROWS)
+        real, imag = azimuth_image(
+            got_second.at[:, :, rows, :], spec.at[1], left_ref, right_ref, twist_ref
+        )
+        source = lax.broadcasted_iota(jnp.int32, real.shape, 1) - offset_ref[0]
+        inside = (source >= 0) & (source < lines)
+        real, imag = jnp.where(inside, real, 0.0), jnp.where(inside, imag, 0.0)
+        first_real, first_imag = image[0, rows, :], image[1, rows, :]
+        place = lax.rem(group + groups - 1, groups)
+        held = pl.ds(pl.multiple_of(ROWS + place * ROWS, ROWS), ROWS)
+        sums[0, held, :] = azimuth_box(first_real * real + first_imag * imag)
+        sums[1, held, :] = azimuth_box(first_imag * real - first_real * imag)
+        sums[2, held, :] = azimuth_box(first_real * first_real + first_imag * first_imag)
+        sums[3, held, :] = azimuth_box(real * real + imag * imag)
+
+        @pl.when(group == 0)
+        def _():
+            for part in range(4):
+                edge_sent[0, 4 * part : 4 * part + 4, :] = sums[part, ROWS + bins - 4 : ROWS + bins]
+
+            @pl.when(me < last)
+            def _():
+                edge_copy(0, me + 1).start()
+
+        @pl.when(group == 1)
+        def _():
+            for part in range(4):
+                edge_sent[1, 4 * part : 4 * part + 4, :] = sums[part, ROWS : ROWS + 4]
+
+            @pl.when(me > 0)
+            def _():
+                edge_copy(1, me - 1).start()
+
+            send_second(early, groups)
+
+        @pl.when(group >= 3)
+        def _():
+            finish(group - 2)
+
+        @pl.when(group == groups - 2)
+        def _():
+            @pl.when(me > 0)
+            def _():
+                edge_copy(0, me - 1).wait_recv()
+                for part in range(4):
+                    sums[part, 4:8, :] = edge_got[0, 4 * part : 4 * part + 4, :]
+
+            @pl.when(me < last)
+            def _():
+                edge_copy(1, me + 1).wait_recv()
+                for part in range(4):
+                    sums[part, ROWS + bins : ROWS + bins + 4, :] = edge_got[
+                        1, 4 * part : 4 * part + 4, :
+                    ]
+
+            finish(0)
+
+        return carry
+
+    lax.fori_loop(0, groups, second_group, 0)
+    finish(groups - 2)
+    finish(groups - 1)
+
+    def first_left(item, carry):
+        piece, dest = item // last, lax.rem(me + 1 + lax.rem(item, last), parts)
+        first_copy(piece, dest, me).wait_send()
+        return carry
+
+    lax.fori_loop(0, halves * last, first_left, 0)
+
+    def second_left(item, carry):
+        group, dest = item // last, lax.rem(me + 1 + lax.rem(item, last), parts)
+        second_copy(group, dest, me).wait_send()
+        return carry
+
+    lax.fori_loop(0, groups * last, second_left, 0)
+
+    @pl.when(me < last)
+    def _():
+        edge_copy(0, me + 1).wait_send()
+
+    @pl.when(me > 0)
+    def _():
+        edge_copy(1, me - 1).wait_send()
+
+    def stored(group, carry):
+        for copy in out_copies(group):
+            copy.wait()
+        return carry
+
+    lax.fori_loop(0, groups, stored, 0)
+
+
+def fits(parts, lines_count, range_count):
+    lines = parts * lines_count
+    bins = WINDOW // parts
+    return (
+        lines_count % TILE == 0
+        and lines & (lines - 1) == 0
+        and lines // LANES == LANES // 2
+        and bins % ROWS == 0
+        and bins >= 6 * ROWS
+        and TILE % bins == 0
+        and parts % 2 == 0
+        and range_count >= WINDOW + (min(range_count, lines) // 4) + 2 * TILE
+    )
+
+
+def on_device(raw_first, raw_second, offsets, chirp_lengths):
+    parts = lax.axis_size("az")
+    lines_count, range_count = raw_first.shape[1:]
+    if not fits(parts, lines_count, range_count):
+        return staged_on_device(raw_first, raw_second, offsets, chirp_lengths)
+    lines = parts * lines_count
+    bins = WINDOW // parts
+    groups, halves = bins // ROWS, lines_count // TILE
+    taps = min(range_count, lines) // 4 // TILE + 1
+    depth = (taps + 1) * TILE
+    left, right, twist = host_tables(lines)
+    vmem = pl.BlockSpec(memory_space=pltpu.VMEM)
+    smem = pl.BlockSpec(memory_space=pltpu.SMEM)
+    hbm = pl.BlockSpec(memory_space=pl.ANY)
+    shared = pltpu.VMEM((parts, 2, bins, lines_count), jnp.float32)
+    dma = pltpu.SemaphoreType.DMA
+    return pl.pallas_call(
+        functools.partial(fused_kernel, parts, taps),
+        out_shape=(
+            jax.ShapeDtypeStruct((2, bins, lines), jnp.float32),
+            jax.ShapeDtypeStruct((bins, lines), jnp.float32),
+        ),
+        in_specs=[smem, smem, hbm, hbm, vmem, vmem, vmem],
+        out_specs=(hbm, hbm),
+        scratch_shapes=[
+            pltpu.VMEM((2, lines_count, WINDOW - TILE + depth), jnp.bfloat16),
+            pltpu.VMEM((4, depth, 2 * TILE), jnp.bfloat16),
+            pltpu.VMEM((2, (taps + ROWS) // ROWS * ROWS, 2 * TILE), jnp.float32),
+            pltpu.VMEM((2, 2, lines // LANES, LANES), jnp.float32),
+            shared,
+            shared,
+            shared,
+            shared,
+            pltpu.VMEM((2, bins, lines), jnp.float32),
+            pltpu.VMEM((4, bins + 2 * ROWS, lines), jnp.float32),
+            pltpu.VMEM((2, 16, lines), jnp.float32),
+            pltpu.VMEM((2, 16, lines), jnp.float32),
+            pltpu.VMEM((2, bins, lines), jnp.float32),
+            pltpu.VMEM((bins, lines), jnp.float32),
+            dma((1,)),
+            dma((halves, parts)),
+            dma((halves, parts)),
+            dma((groups, parts)),
+            dma((groups, parts)),
+            dma((2,)),
+            dma((2,)),
+            dma((2, groups)),
+        ],
+        compiler_params=pltpu.CompilerParams(
+            collective_id=0, has_side_effects=True, vmem_limit_bytes=67043328
+        ),
+        name="fused",
+    )(offsets, chirp_lengths, raw_first, raw_second, left, right, twist)
+
+
 def solution(mesh):
     in_specs = (P("groups", "az", None), P("groups", "az", None), P("groups"), P("groups"))
     out_specs = (P("groups", "az", None), P(("groups", "az"), None))

time: 287 us -> 218 us (0.76); the launches traced: 282 us -> 218 us
  waiting for transfers between devices: 137 us -> 0 us
  Pallas kernels: 106 us -> 211 us
  starting transfers between devices: 17.8 us -> 0 us
  other arithmetic: 10.6 us -> 0 us
  between operations: 4.53 us -> 0.65 us
    all_to_all x2 -> x0, waiting for transfers between devices: 131 us -> none  [the longest x1 68.1 us: on_device(): lax.all_to_all(second_ranged, 'az', split_axis=0, concat_axis=0, tiled=True)]
    pallas_call x5 -> x1, Pallas kernels: 106 us -> 211 us  [on_device(): pl.pallas_call(functools.partial(fused_kernel, parts, taps), out_shape=(j...]
    all_to_all x2 -> x0, starting transfers between devices: 11.3 us -> none  [the longest x1 6.52 us: on_device(): lax.all_to_all(first_ranged, 'az', split_axis=0, concat_axis=0, tiled=True)]
    ppermute x2 -> x0, starting transfers between devices: 6.46 us -> none  [the longest x1 4.44 us: neighbours(): lax.ppermute(block[:, -width:], axis, ahead)]
    ppermute x2 -> x0, waiting for transfers between devices: 6.15 us -> none  [the longest x1 5.02 us: neighbours(): lax.ppermute(block[:, :width], axis, back)]
    unnamed x6 -> x4, local copies, waits for them, and re-layouts: 0.87 us -> 6.08 us
    slice x3 -> x0, local copies, waits for them, and re-layouts: 4.41 us -> none  [the longest x1 1.72 us: neighbours(): block[:, :width]]
    mul x5 -> x0, other arithmetic: 3.85 us -> none  [the longest x1 2.77 us: chirp_segments(): amplitude * jnp.cos(angles)]
  transfers between devices with their start and end apart: 4 -> 0, of which waited for: 4 -> 0; matrix products, arithmetic and copies ran while one was open for 3% -> 0% of each run, Pallas kernels for 16% -> 0%
where the time goes in v1:
time: 218 us
  Pallas kernels  211 us (97%)
  local copies, waits for them, and re-layouts  6.08 us (3%)
    pallas_call x1, Pallas kernels, on_device(): pl.pallas_call(functools.partial(fused_kernel, parts, taps), out_shape=(j...  211 us
    unnamed x4, local copies, waits for them, and re-layouts  6.08 us

profile of v1, /device:TPU:15, one launch (start us, length us, event | category | flops | bytes accessed | tf_op | source)
XLA Modules:
  0.0 218.1 jit_solution(6447583339364248069)
XLA Ops:
  0.6 211.4 %fused.1 = (f32[2,64,8192]{2,1,0:T(8,128)}, f32[64,8192]{1,0:T(8,128)}) custom-call(s32[2]{0:T(128)} %offset_ref.1, s32[2]{0:T(128)} %length_ref.1, bf16[2,512,8192]{2,1,0:T(8,128)(2,1)} %raw_first.1, bf16[2,512,8192]{2,1,0:T(8,128)(2,1)} %raw_second.1, bf16[4,128,128]{2,1,0:T(8,128)(2,1)} %constant.6.clone.left_ref, ...), custom_call_target="tpu_custom_call" | custom-call | tf_op jit(solution)/shard_map/fused/pallas_call | solution.py:872
  212.0 0.0 copy-start
  212.0 4.8 %copy.11 = f32[2,64,8192]{2,1,0:T(8,128)} copy(f32[2,64,8192]{2,1,0:T(8,128)} %get-tuple-element.4) | data formatting | bytes 8388608
  216.8 0.0 copy-done
  216.8 1.3 copy.12
Async XLA Ops:
  212.0 4.8 %copy-start = (f32[64,8192]{1,0:T(8,128)S(1)}, f32[64,8192]{1,0:T(8,128)}, u32[]{:S(2)}) copy-start(f32[64,8192]{1,0:T(8,128)} %get-tuple-element.5) | copy-start | bytes 6291460

commit v2 on v1

--- a/solution.py
+++ b/solution.py
@@ -549,11 +549,11 @@
 def fused_kernel(
     parts, taps,
     offset_ref, length_ref, raw_first, raw_second, left_ref, right_ref, twist_ref,
-    inter_ref, coherence_ref,
-    raw, tab, seg, spec, sent_first, sent_second, got_first, got_second, image, sums,
-    edge_sent, edge_got, inter_out, coherence_out,
-    raw_sem, first_send, first_recv, second_send, second_recv, edge_send_sem, edge_recv_sem,
-    out_sem,
+    inter_out, coherence_out,
+    raw, tab, seg, spec, sent_first, sent_second, got_first, got_second, image, windows,
+    running, outer, edge_sent, edge_got,
+    raw_sem, first_send, first_recv, second_send, second_recv, halo_send, halo_recv,
+    edge_send_sem, edge_recv_sem,
 ):
     me = lax.axis_index("az")
     bins, lines_count = sent_first.shape[2], sent_first.shape[3]
@@ -563,14 +563,20 @@
     blocks = WINDOW // TILE
     per_block = TILE // bins
     last = parts - 1
-
-    def load(source):
+    middle = parts // 2
+    extra = jnp.where((me == middle) | (me == middle - 1), 1, 0)
+
+    def load(source, piece):
         width = raw.shape[2] - LANES
+        rows = pl.ds(pl.multiple_of(piece * TILE, TILE), TILE)
         return pltpu.make_async_copy(
-            source.at[:, :, pl.ds(0, width)], raw.at[:, :, pl.ds(LANES, width)], raw_sem.at[0]
-        )
-
-    load(raw_first).start()
+            source.at[:, rows, pl.ds(0, width)],
+            raw.at[:, rows, pl.ds(LANES, width)],
+            raw_sem.at[piece],
+        )
+
+    for piece in range(halves):
+        load(raw_first, piece).start()
     barrier = pltpu.get_barrier_semaphore()
 
     def greet(step, carry):
@@ -580,7 +586,6 @@
     lax.fori_loop(1, parts, greet, 0)
     raw[:, :, 0:LANES] = jnp.zeros((2, lines_count, LANES), jnp.bfloat16)
     build_table(taps, 0, length_ref[0], seg, tab)
-    load(raw_first).wait()
     pl.semaphore_wait(barrier, parts - 1)
 
     half = me // (parts // 2)
@@ -612,7 +617,7 @@
         rows = pl.ds(pl.multiple_of(piece * TILE, TILE), TILE)
         return pltpu.make_async_remote_copy(
             src_ref=sent_first.at[dest, :, :, rows],
-            dst_ref=got_first.at[source, :, :, rows],
+            dst_ref=got_first.at[source, :, pl.ds(0, bins), rows],
             send_sem=first_send.at[piece, dest],
             recv_sem=first_recv.at[piece, source],
             device_id={"az": dest},
@@ -620,6 +625,11 @@
 
     def first_tile(step, carry):
         block, piece = block_of(step // halves), lax.rem(step, halves)
+
+        @pl.when(step < halves)
+        def _():
+            load(raw_first, piece).wait()
+
         correlate(block, piece, LANES, taps * TILE, sent_first, None)
 
         def send(item, inner):
@@ -636,9 +646,58 @@
 
     lax.fori_loop(0, blocks * halves, first_tile, 0)
 
-    load(raw_second).start()
+    for piece in range(halves):
+        load(raw_second, piece).start()
+
+    def halo_copy(number, side, source):
+        sent, got = ((sent_first, got_first), (sent_second, got_second))[number]
+        owner, start, place = ((middle, ROWS, 0), (middle - 1, ROWS // 2, ROWS // 2))[side]
+        return pltpu.make_async_remote_copy(
+            src_ref=sent.at[owner, :, pl.ds(start, ROWS // 2), :],
+            dst_ref=got.at[source, :, pl.ds(bins + place, ROWS // 2), :],
+            send_sem=halo_send.at[number, side],
+            recv_sem=halo_recv.at[number, source],
+            device_id={"az": middle - 1 + side},
+        )
+
+    def send_halo(number):
+        sent, got = ((sent_first, got_first), (sent_second, got_second))[number]
+        for side in range(2):
+            @pl.when(me != middle - 1 + side)
+            def _():
+                halo_copy(number, side, me).start()
+
+        half_rows = ROWS // 2
+
+        @pl.when(me == middle - 1)
+        def _():
+            got[me, :, bins : bins + half_rows, :] = sent[middle, :, ROWS : ROWS + half_rows, :]
+
+        @pl.when(me == middle)
+        def _():
+            got[me, :, bins + half_rows : bins + ROWS, :] = sent[middle - 1, :, half_rows:ROWS, :]
+
+    def halo_arrived(number):
+        for side in range(2):
+            @pl.when(me == middle - 1 + side)
+            def _():
+                def one(step, carry):
+                    source = lax.rem(me + step, parts)
+                    halo_copy(number, side, source).wait_recv()
+                    return carry
+
+                lax.fori_loop(1, parts, one, 0)
+
+    def halo_left(number):
+        for side in range(2):
+            @pl.when(me != middle - 1 + side)
+            def _():
+                halo_copy(number, side, me).wait_send()
+
+    send_halo(0)
     build_table(taps + 1, offset_ref[1] - LANES, length_ref[0], seg, tab)
-    load(raw_second).wait()
+    for piece in range(halves):
+        load(raw_second, piece).wait()
 
     def second_tile(step, carry):
         correlate(
@@ -668,11 +727,11 @@
         lax.fori_loop(0, (stop - start) * last, send, 0)
 
     early = groups // 2
+    send_halo(1)
     send_second(0, early)
-    got_first[me] = sent_first[me]
-    got_second[me] = sent_second[me]
-    sums[:, 0:ROWS, :] = jnp.zeros((4, ROWS, lines), jnp.float32)
-    sums[:, pl.ds(ROWS + bins, ROWS), :] = jnp.zeros((4, ROWS, lines), jnp.float32)
+    got_first[me, :, 0:bins, :] = sent_first[me]
+    got_second[me, :, 0:bins, :] = sent_second[me]
+    running[...] = jnp.zeros((4, ROWS, lines), jnp.float32)
     azimuth_filter(length_ref[1], offset_ref[0], lines, left_ref, right_ref, twist_ref, spec)
 
     def first_arrived(item, carry):
@@ -681,6 +740,7 @@
         return carry
 
     lax.fori_loop(0, halves * last, first_arrived, 0)
+    halo_arrived(0)
 
     def first_group(group, carry):
         rows = pl.ds(pl.multiple_of(group * ROWS, ROWS), ROWS)
@@ -691,7 +751,7 @@
         image[1, rows, :] = imag
         return carry
 
-    lax.fori_loop(0, groups, first_group, 0)
+    lax.fori_loop(0, groups + extra, first_group, 0)
 
     def edge_copy(side, dest):
         return pltpu.make_async_remote_copy(
@@ -702,50 +762,53 @@
             device_id={"az": dest},
         )
 
-    def out_copies(group):
-        rows = pl.ds(pl.multiple_of(group * ROWS, ROWS), ROWS)
-        return (
-            pltpu.make_async_copy(
-                inter_out.at[:, rows, :], inter_ref.at[:, rows, :], out_sem.at[0, group]
-            ),
-            pltpu.make_async_copy(
-                coherence_out.at[rows, :], coherence_ref.at[rows, :], out_sem.at[1, group]
-            ),
-        )
-
-    width = 4 * LANES
+    row = lax.broadcasted_iota(jnp.int32, (ROWS, lines), 0)
+
+    def scans(values):
+        before = jnp.where(row >= 1, pltpu.roll(values, 1, 0), 0.0)
+        after = values
+        for step in (1, 2, 4):
+            before = before + jnp.where(row >= step, pltpu.roll(before, step, 0), 0.0)
+            after = after + jnp.where(
+                row < ROWS - step, pltpu.roll(after, ROWS - step, 0), 0.0
+            )
+        return before, after
+
+    def band(group):
+        return pl.ds(pl.multiple_of(group * ROWS, ROWS), ROWS)
 
     def finish(group):
-        start = group * ROWS
-
-        def piece(item, carry):
-            columns = pl.ds(pl.multiple_of(item * width, width), width)
-            boxes = []
-            for part in range(4):
-                held = sums[part, pl.ds(pl.multiple_of(start, ROWS), 3 * ROWS), columns]
-                for step in (1, 2, 4):
-                    held = held + pltpu.roll(held, 3 * ROWS - step, 0)
-                boxes.append(pltpu.roll(held, 3 * ROWS - 5, 0)[0:ROWS])
-            rows = pl.ds(pl.multiple_of(start, ROWS), ROWS)
-            inter_out[0, rows, columns] = boxes[0] * (1.0 / 64.0)
-            inter_out[1, rows, columns] = boxes[1] * (1.0 / 64.0)
-            coherence_out[rows, columns] = jnp.sqrt(
-                boxes[0] * boxes[0] + boxes[1] * boxes[1]
-            ) / jnp.sqrt(boxes[2] * boxes[3] + 1.0)
-            return carry
-
-        lax.fori_loop(0, lines // width, piece, 0)
-        for copy in out_copies(group):
-            copy.start()
-
-    def second_group(group, carry):
-        def arrived(step, inner):
-            source = lax.rem(me + step, parts)
-            second_copy(group, source, source).wait_recv()
-            return inner
-
-        lax.fori_loop(1, parts, arrived, 0)
-        rows = pl.ds(pl.multiple_of(group * ROWS, ROWS), ROWS)
+        rows = band(group)
+        later = lax.broadcasted_iota(jnp.int32, (ROWS, lines), 0) >= 5
+        boxes = [
+            pltpu.roll(
+                jnp.where(later, windows[part, rows, :], windows[part, band(group + 1), :]), 3, 0
+            )
+            for part in range(4)
+        ]
+        inter_out[0, rows, :] = boxes[0] * (1.0 / 64.0)
+        inter_out[1, rows, :] = boxes[1] * (1.0 / 64.0)
+        coherence_out[rows, :] = jnp.sqrt(boxes[0] * boxes[0] + boxes[1] * boxes[1]) / jnp.sqrt(
+            boxes[2] * boxes[3] + 1.0
+        )
+
+    def second_group(item, carry):
+        group = lax.rem(item + groups + 1, groups + 1)
+
+        @pl.when(item >= 0)
+        def _():
+            def arrived(step, inner):
+                source = lax.rem(me + step, parts)
+                second_copy(group, source, source).wait_recv()
+                return inner
+
+            lax.fori_loop(1, parts, arrived, 0)
+
+        @pl.when(item < 0)
+        def _():
+            halo_arrived(1)
+
+        rows = band(group)
         real, imag = azimuth_image(
             got_second.at[:, :, rows, :], spec.at[1], left_ref, right_ref, twist_ref
         )
@@ -753,50 +816,81 @@
         inside = (source >= 0) & (source < lines)
         real, imag = jnp.where(inside, real, 0.0), jnp.where(inside, imag, 0.0)
         first_real, first_imag = image[0, rows, :], image[1, rows, :]
-        place = lax.rem(group + groups - 1, groups)
-        held = pl.ds(pl.multiple_of(ROWS + place * ROWS, ROWS), ROWS)
-        sums[0, held, :] = azimuth_box(first_real * real + first_imag * imag)
-        sums[1, held, :] = azimuth_box(first_imag * real - first_real * imag)
-        sums[2, held, :] = azimuth_box(first_real * first_real + first_imag * first_imag)
-        sums[3, held, :] = azimuth_box(real * real + imag * imag)
-
-        @pl.when(group == 0)
+        products = (
+            first_real * real + first_imag * imag,
+            first_imag * real - first_real * imag,
+            first_real * first_real + first_imag * first_imag,
+            real * real + imag * imag,
+        )
+        for part in range(4):
+            before, after = scans(azimuth_box(products[part]))
+            outer[0, part] = before
+            outer[1, part] = after
+
+        @pl.when(item < 0)
         def _():
             for part in range(4):
-                edge_sent[0, 4 * part : 4 * part + 4, :] = sums[part, ROWS + bins - 4 : ROWS + bins]
-
-            @pl.when(me < last)
+                low, high = 4 * part, 4 * part + 4
+
+                @pl.when(me == middle)
+                def _():
+                    edge_got[0, low:high, :] = outer[1, part, 4:8, :]
+
+                @pl.when(me != middle)
+                def _():
+                    edge_got[1, low:high, :] = outer[0, part, 1:5, :]
+
+        @pl.when(item == 0)
+        def _():
+            for part in range(4):
+                edge_sent[0, 4 * part : 4 * part + 4, :] = outer[1, part, 4:8, :]
+                windows[part, bins - ROWS : bins, :] = outer[0, part]
+                windows[part, bins : bins + ROWS, :] = outer[1, part]
+
+            @pl.when((me < last) & (me != middle - 1))
             def _():
                 edge_copy(0, me + 1).start()
 
-        @pl.when(group == 1)
+        @pl.when(item >= 1)
         def _():
             for part in range(4):
-                edge_sent[1, 4 * part : 4 * part + 4, :] = sums[part, ROWS : ROWS + 4]
-
-            @pl.when(me > 0)
+                windows[part, band(item - 1), :] = running[part] + outer[0, part]
+                running[part] = outer[1, part]
+
+        @pl.when(item == 1)
+        def _():
+            for part in range(4):
+                edge_sent[1, 4 * part : 4 * part + 4, :] = outer[0, part, 1:5, :]
+
+            @pl.when((me > 0) & (me != middle))
             def _():
                 edge_copy(1, me - 1).start()
 
             send_second(early, groups)
 
-        @pl.when(group >= 3)
+        @pl.when(item >= 3)
         def _():
-            finish(group - 2)
-
-        @pl.when(group == groups - 2)
+            finish(item - 2)
+
+        @pl.when(item == groups - 2)
         def _():
             @pl.when(me > 0)
             def _():
-                edge_copy(0, me - 1).wait_recv()
+                @pl.when(me != middle)
+                def _():
+                    edge_copy(0, me - 1).wait_recv()
+
                 for part in range(4):
-                    sums[part, 4:8, :] = edge_got[0, 4 * part : 4 * part + 4, :]
+                    windows[part, 4:8, :] += edge_got[0, 4 * part : 4 * part + 4, :]
 
             @pl.when(me < last)
             def _():
-                edge_copy(1, me + 1).wait_recv()
+                @pl.when(me != middle - 1)
+                def _():
+                    edge_copy(1, me + 1).wait_recv()
+
                 for part in range(4):
-                    sums[part, ROWS + bins : ROWS + bins + 4, :] = edge_got[
+                    windows[part, bins + 1 : bins + 5, :] += edge_got[
                         1, 4 * part : 4 * part + 4, :
                     ]
 
@@ -804,7 +898,9 @@
 
         return carry
 
-    lax.fori_loop(0, groups, second_group, 0)
+    lax.fori_loop(0 - extra, groups, second_group, 0)
+    for part in range(4):
+        windows[part, bins - ROWS : bins, :] += running[part]
     finish(groups - 2)
     finish(groups - 1)
 
@@ -822,20 +918,27 @@
 
     lax.fori_loop(0, groups * last, second_left, 0)
 
-    @pl.when(me < last)
+    halo_left(0)
+    halo_left(1)
+
+    @pl.when((me < last) & (me != middle - 1))
     def _():
         edge_copy(0, me + 1).wait_send()
 
-    @pl.when(me > 0)
+    @pl.when((me > 0) & (me != middle))
     def _():
         edge_copy(1, me - 1).wait_send()
 
-    def stored(group, carry):
-        for copy in out_copies(group):
-            copy.wait()
-        return carry
-
-    lax.fori_loop(0, groups, stored, 0)
+
+def store_kernel(inter_ref, coherence_ref, inter_out, coherence_out, sems):
+    copies = [
+        pltpu.make_async_copy(inter_ref, inter_out, sems.at[0]),
+        pltpu.make_async_copy(coherence_ref, coherence_out, sems.at[1]),
+    ]
+    for copy in copies:
+        copy.start()
+    for copy in copies:
+        copy.wait()
 
 
 def fits(parts, lines_count, range_count):
@@ -867,45 +970,59 @@
     vmem = pl.BlockSpec(memory_space=pltpu.VMEM)
     smem = pl.BlockSpec(memory_space=pltpu.SMEM)
     hbm = pl.BlockSpec(memory_space=pl.ANY)
-    shared = pltpu.VMEM((parts, 2, bins, lines_count), jnp.float32)
+    sent = pltpu.VMEM((parts, 2, bins, lines_count), jnp.float32)
+    got = pltpu.VMEM((parts, 2, bins + ROWS, lines_count), jnp.float32)
     dma = pltpu.SemaphoreType.DMA
-    return pl.pallas_call(
+    held = pl.pallas_call(
         functools.partial(fused_kernel, parts, taps),
         out_shape=(
-            jax.ShapeDtypeStruct((2, bins, lines), jnp.float32),
-            jax.ShapeDtypeStruct((bins, lines), jnp.float32),
+            pltpu.VMEM((2, bins, lines), jnp.float32),
+            pltpu.VMEM((bins, lines), jnp.float32),
         ),
         in_specs=[smem, smem, hbm, hbm, vmem, vmem, vmem],
-        out_specs=(hbm, hbm),
+        out_specs=(vmem, vmem),
         scratch_shapes=[
             pltpu.VMEM((2, lines_count, WINDOW - TILE + depth), jnp.bfloat16),
             pltpu.VMEM((4, depth, 2 * TILE), jnp.bfloat16),
             pltpu.VMEM((2, (taps + ROWS) // ROWS * ROWS, 2 * TILE), jnp.float32),
             pltpu.VMEM((2, 2, lines // LANES, LANES), jnp.float32),
-            shared,
-            shared,
-            shared,
-            shared,
-            pltpu.VMEM((2, bins, lines), jnp.float32),
-            pltpu.VMEM((4, bins + 2 * ROWS, lines), jnp.float32),
+            sent,
+            sent,
+            got,
+            got,
+            pltpu.VMEM((2, bins + ROWS, lines), jnp.float32),
+            pltpu.VMEM((4, bins + ROWS, lines), jnp.float32),
+            pltpu.VMEM((4, ROWS, lines), jnp.float32),
+            pltpu.VMEM((2, 4, ROWS, lines), jnp.float32),
             pltpu.VMEM((2, 16, lines), jnp.float32),
             pltpu.VMEM((2, 16, lines), jnp.float32),
-            pltpu.VMEM((2, bins, lines), jnp.float32),
-            pltpu.VMEM((bins, lines), jnp.float32),
-            dma((1,)),
+            dma((halves,)),
             dma((halves, parts)),
             dma((halves, parts)),
             dma((groups, parts)),
             dma((groups, parts)),
+            dma((2, 2)),
+            dma((2, parts)),
             dma((2,)),
             dma((2,)),
-            dma((2, groups)),
         ],
         compiler_params=pltpu.CompilerParams(
-            collective_id=0, has_side_effects=True, vmem_limit_bytes=67043328
+            collective_id=0, has_side_effects=True, vmem_limit_bytes=57 * 1024 * 1024
         ),
         name="fused",
     )(offsets, chirp_lengths, raw_first, raw_second, left, right, twist)
+    return pl.pallas_call(
+        store_kernel,
+        out_shape=(
+            jax.ShapeDtypeStruct((2, bins, lines), jnp.float32),
+            jax.ShapeDtypeStruct((bins, lines), jnp.float32),
+        ),
+        in_specs=[vmem, vmem],
+        out_specs=(hbm, hbm),
+        scratch_shapes=[dma((2,))],
+        compiler_params=pltpu.CompilerParams(vmem_limit_bytes=1024 * 1024),
+        name="store",
+    )(*held)
 
 
 def solution(mesh):

time: 218 us -> 204 us (0.936)
  Pallas kernels: 211 us -> 203 us
  local copies, waits for them, and re-layouts: 6.08 us -> 0 us
    pallas_call x1 -> x2, Pallas kernels: 211 us -> 203 us  [the longest x1 201 us: on_device(): pl.pallas_call(functools.partial(fused_kernel, parts, taps), out_shape=(p...]
    unnamed x4 -> x0, local copies, waits for them, and re-layouts: 6.08 us -> none
where the time goes in v2:
time: 204 us
  Pallas kernels  203 us (100%)
    pallas_call x1, Pallas kernels, on_device(): pl.pallas_call(functools.partial(fused_kernel, parts, taps), out_shape=(p...  201 us

profile of v2, /device:TPU:15, one launch (start us, length us, event | category | flops | bytes accessed | tf_op | source)
XLA Modules:
  0.0 204.3 jit_solution(12113028271058333646)
XLA Ops:
  0.6 200.8 %fused.1 = (f32[2,64,8192]{2,1,0:T(8,128)S(1)}, f32[64,8192]{1,0:T(8,128)S(1)}) custom-call(s32[2]{0:T(128)} %offset_ref.1, s32[2]{0:T(128)} %length_ref.1, bf16[2,512,8192]{2,1,0:T(8,128)(2,1)} %raw_first.1, bf16[2,512,8192]{2,1,0:T(8,128)(2,1)} %raw_second.1, bf16[4,128,128]{2,1,0:T(8,128)(2,1)} %constant.6.clone.left_ref, ...), custom_call_target="tpu_custom_call" | custom-call | tf_op jit(solution)/shard_map/fused/pallas_call | solution.py:976
  201.4 2.7 %store.1 = (f32[2,64,8192]{2,1,0:T(8,128)}, f32[64,8192]{1,0:T(8,128)}) custom-call(f32[2,64,8192]{2,1,0:T(8,128)S(1)} %get-tuple-element.4.inter_ref, f32[64,8192]{1,0:T(8,128)S(1)} %get-tuple-element.5.coherence_ref), custom_call_target="tpu_custom_call" | custom-call | tf_op jit(solution)/shard_map/store/pallas_call | solution.py:1014

commit v3 on v2

--- a/solution.py
+++ b/solution.py
@@ -549,10 +549,10 @@
 def fused_kernel(
     parts, taps,
     offset_ref, length_ref, raw_first, raw_second, left_ref, right_ref, twist_ref,
-    inter_out, coherence_out,
-    raw, tab, seg, spec, sent_first, sent_second, got_first, got_second, image, windows,
-    running, outer, edge_sent, edge_got,
-    raw_sem, first_send, first_recv, second_send, second_recv, halo_send, halo_recv,
+    inter_out, coherence_out, windows, running,
+    raw, tab, seg, spec, sent_first, sent_second, got_first, got_second, image, power,
+    outer, edge_sent, edge_got,
+    raw_sem, first_sem, second_send, second_recv, halo_send, halo_recv,
     edge_send_sem, edge_recv_sem,
 ):
     me = lax.axis_index("az")
@@ -560,6 +560,7 @@
     lines = parts * lines_count
     groups = bins // ROWS
     halves = lines_count // TILE
+    pieces = lines_count // LANES
     blocks = WINDOW // TILE
     per_block = TILE // bins
     last = parts - 1
@@ -568,14 +569,14 @@
 
     def load(source, piece):
         width = raw.shape[2] - LANES
-        rows = pl.ds(pl.multiple_of(piece * TILE, TILE), TILE)
+        rows = pl.ds(pl.multiple_of(piece * LANES, LANES), LANES)
         return pltpu.make_async_copy(
             source.at[:, rows, pl.ds(0, width)],
             raw.at[:, rows, pl.ds(LANES, width)],
             raw_sem.at[piece],
         )
 
-    for piece in range(halves):
+    for piece in range(pieces):
         load(raw_first, piece).start()
     barrier = pltpu.get_barrier_semaphore()
 
@@ -595,8 +596,8 @@
         side = lax.rem(half + 1 + step // (blocks // 2), 2)
         return side * (blocks // 2) + lax.rem(step + turn, blocks // 2)
 
-    def correlate(block, piece, start, depth, target, low):
-        rows = pl.ds(pl.multiple_of(piece * TILE, TILE), TILE)
+    def correlate(block, piece, height, start, depth, target, low):
+        rows = pl.ds(pl.multiple_of(piece * height, height), height)
         columns = pl.ds(pl.multiple_of(start + block * TILE, LANES), depth)
         real, imag = raw[0, rows, columns], raw[1, rows, columns]
         table = pl.ds(0, depth)
@@ -606,47 +607,56 @@
         for part in range(2):
             turned = result[:, part * TILE : (part + 1) * TILE].T
             if low is not None:
-                place = block * TILE + lax.broadcasted_iota(jnp.int32, (TILE, TILE), 0)
+                place = block * TILE + lax.broadcasted_iota(jnp.int32, (TILE, height), 0)
                 turned = jnp.where(place >= low, turned, 0.0)
-            turned = turned.reshape(per_block, bins, TILE)
+            turned = turned.reshape(per_block, bins, height)
             where = pl.ds(block * per_block, per_block)
             target[where, part, ROWS:bins, rows] = turned[:, 0 : bins - ROWS]
             target[where, part, 0:ROWS, rows] = turned[:, bins - ROWS : bins]
 
-    def first_copy(piece, dest, source):
-        rows = pl.ds(pl.multiple_of(piece * TILE, TILE), TILE)
+    def first_copy(piece, dest):
+        rows = pl.ds(pl.multiple_of(piece * LANES, LANES), LANES)
         return pltpu.make_async_remote_copy(
             src_ref=sent_first.at[dest, :, :, rows],
-            dst_ref=got_first.at[source, :, pl.ds(0, bins), rows],
-            send_sem=first_send.at[piece, dest],
-            recv_sem=first_recv.at[piece, source],
+            dst_ref=got_first.at[me, :, pl.ds(0, bins), rows],
+            send_sem=first_sem.at[0],
+            recv_sem=first_sem.at[1],
             device_id={"az": dest},
         )
 
+    def first_whole():
+        return pltpu.make_async_remote_copy(
+            src_ref=sent_first.at[pl.ds(0, last)],
+            dst_ref=got_first.at[pl.ds(0, last), :, pl.ds(0, bins), :],
+            send_sem=first_sem.at[0],
+            recv_sem=first_sem.at[1],
+            device_id={"az": lax.rem(me + 1, parts)},
+        )
+
     def first_tile(step, carry):
-        block, piece = block_of(step // halves), lax.rem(step, halves)
-
-        @pl.when(step < halves)
+        block, piece = block_of(step // pieces), lax.rem(step, pieces)
+
+        @pl.when(step < pieces)
         def _():
             load(raw_first, piece).wait()
 
-        correlate(block, piece, LANES, taps * TILE, sent_first, None)
+        correlate(block, piece, LANES, LANES, taps * TILE, sent_first, None)
 
         def send(item, inner):
             dest = block * per_block + lax.rem(item + me, per_block)
 
             @pl.when(dest != me)
             def _():
-                first_copy(piece, dest, me).start()
+                first_copy(piece, dest).start()
 
             return inner
 
         lax.fori_loop(0, per_block, send, 0)
         return carry
 
-    lax.fori_loop(0, blocks * halves, first_tile, 0)
-
-    for piece in range(halves):
+    lax.fori_loop(0, blocks * pieces, first_tile, 0)
+
+    for piece in range(pieces):
         load(raw_second, piece).start()
 
     def halo_copy(number, side, source):
@@ -696,32 +706,42 @@
 
     send_halo(0)
     build_table(taps + 1, offset_ref[1] - LANES, length_ref[0], seg, tab)
-    for piece in range(halves):
+    for piece in range(pieces):
         load(raw_second, piece).wait()
 
     def second_tile(step, carry):
         correlate(
-            step // halves, lax.rem(step, halves), 0, (taps + 1) * TILE, sent_second,
+            step // halves, lax.rem(step, halves), TILE, 0, (taps + 1) * TILE, sent_second,
             offset_ref[1],
         )
         return carry
 
     lax.fori_loop(0, blocks * halves, second_tile, 0)
 
-    def second_copy(group, dest, source):
+    def second_copy(group, dest):
         rows = pl.ds(pl.multiple_of(group * ROWS, ROWS), ROWS)
         return pltpu.make_async_remote_copy(
             src_ref=sent_second.at[dest, :, rows, :],
-            dst_ref=got_second.at[source, :, rows, :],
-            send_sem=second_send.at[group, dest],
-            recv_sem=second_recv.at[group, source],
+            dst_ref=got_second.at[me, :, rows, :],
+            send_sem=second_send.at[group],
+            recv_sem=second_recv.at[group],
             device_id={"az": dest},
+        )
+
+    def second_whole(group):
+        rows = pl.ds(pl.multiple_of(group * ROWS, ROWS), ROWS)
+        return pltpu.make_async_remote_copy(
+            src_ref=sent_second.at[pl.ds(0, last), :, rows, :],
+            dst_ref=got_second.at[pl.ds(0, last), :, rows, :],
+            send_sem=second_send.at[group],
+            recv_sem=second_recv.at[group],
+            device_id={"az": lax.rem(me + 1, parts)},
         )
 
     def send_second(start, stop):
         def send(item, carry):
             group, step = start + item // last, 1 + lax.rem(item, last)
-            second_copy(group, lax.rem(me + step, parts), me).start()
+            second_copy(group, lax.rem(me + step, parts)).start()
             return carry
 
         lax.fori_loop(0, (stop - start) * last, send, 0)
@@ -734,12 +754,7 @@
     running[...] = jnp.zeros((4, ROWS, lines), jnp.float32)
     azimuth_filter(length_ref[1], offset_ref[0], lines, left_ref, right_ref, twist_ref, spec)
 
-    def first_arrived(item, carry):
-        piece, source = item // last, lax.rem(me + 1 + lax.rem(item, last), parts)
-        first_copy(piece, source, source).wait_recv()
-        return carry
-
-    lax.fori_loop(0, halves * last, first_arrived, 0)
+    first_whole().wait_recv()
     halo_arrived(0)
 
     def first_group(group, carry):
@@ -749,6 +764,7 @@
         )
         image[0, rows, :] = real
         image[1, rows, :] = imag
+        power[rows, :] = azimuth_box(real * real + imag * imag)
         return carry
 
     lax.fori_loop(0, groups + extra, first_group, 0)
@@ -779,17 +795,9 @@
 
     def finish(group):
         rows = band(group)
-        later = lax.broadcasted_iota(jnp.int32, (ROWS, lines), 0) >= 5
-        boxes = [
-            pltpu.roll(
-                jnp.where(later, windows[part, rows, :], windows[part, band(group + 1), :]), 3, 0
-            )
-            for part in range(4)
-        ]
-        inter_out[0, rows, :] = boxes[0] * (1.0 / 64.0)
-        inter_out[1, rows, :] = boxes[1] * (1.0 / 64.0)
-        coherence_out[rows, :] = jnp.sqrt(boxes[0] * boxes[0] + boxes[1] * boxes[1]) / jnp.sqrt(
-            boxes[2] * boxes[3] + 1.0
+        inter_out[0, rows, :], inter_out[1, rows, :], coherence_out[rows, :] = results(
+            [windows[part, rows, :] for part in range(4)],
+            [windows[part, band(group + 1), :] for part in range(4)],
         )
 
     def second_group(item, carry):
@@ -797,12 +805,7 @@
 
         @pl.when(item >= 0)
         def _():
-            def arrived(step, inner):
-                source = lax.rem(me + step, parts)
-                second_copy(group, source, source).wait_recv()
-                return inner
-
-            lax.fori_loop(1, parts, arrived, 0)
+            second_whole(group).wait_recv()
 
         @pl.when(item < 0)
         def _():
@@ -816,14 +819,14 @@
         inside = (source >= 0) & (source < lines)
         real, imag = jnp.where(inside, real, 0.0), jnp.where(inside, imag, 0.0)
         first_real, first_imag = image[0, rows, :], image[1, rows, :]
-        products = (
-            first_real * real + first_imag * imag,
-            first_imag * real - first_real * imag,
-            first_real * first_real + first_imag * first_imag,
-            real * real + imag * imag,
+        sums = (
+            azimuth_box(first_real * real + first_imag * imag),
+            azimuth_box(first_imag * real - first_real * imag),
+            power[rows, :],
+            azimuth_box(real * real + imag * imag),
         )
         for part in range(4):
-            before, after = scans(azimuth_box(products[part]))
+            before, after = scans(sums[part])
             outer[0, part] = before
             outer[1, part] = after
 
@@ -868,7 +871,7 @@
 
             send_second(early, groups)
 
-        @pl.when(item >= 3)
+        @pl.when((item >= 3) & (item < groups - 1))
         def _():
             finish(item - 2)
 
@@ -899,25 +902,13 @@
         return carry
 
     lax.fori_loop(0 - extra, groups, second_group, 0)
-    for part in range(4):
-        windows[part, bins - ROWS : bins, :] += running[part]
-    finish(groups - 2)
-    finish(groups - 1)
-
-    def first_left(item, carry):
-        piece, dest = item // last, lax.rem(me + 1 + lax.rem(item, last), parts)
-        first_copy(piece, dest, me).wait_send()
+    first_whole().wait_send()
+
+    def second_left(group, carry):
+        second_whole(group).wait_send()
         return carry
 
-    lax.fori_loop(0, halves * last, first_left, 0)
-
-    def second_left(item, carry):
-        group, dest = item // last, lax.rem(me + 1 + lax.rem(item, last), parts)
-        second_copy(group, dest, me).wait_send()
-        return carry
-
-    lax.fori_loop(0, groups * last, second_left, 0)
-
+    lax.fori_loop(0, groups, second_left, 0)
     halo_left(0)
     halo_left(1)
 
@@ -930,15 +921,61 @@
         edge_copy(1, me - 1).wait_send()
 
 
-def store_kernel(inter_ref, coherence_ref, inter_out, coherence_out, sems):
-    copies = [
-        pltpu.make_async_copy(inter_ref, inter_out, sems.at[0]),
-        pltpu.make_async_copy(coherence_ref, coherence_out, sems.at[1]),
-    ]
-    for copy in copies:
+def results(now, then):
+    later = lax.broadcasted_iota(jnp.int32, now[0].shape, 0) >= 5
+    boxes = [pltpu.roll(jnp.where(later, now[part], then[part]), 3, 0) for part in range(4)]
+    coherence = jnp.sqrt(boxes[0] * boxes[0] + boxes[1] * boxes[1]) / jnp.sqrt(
+        boxes[2] * boxes[3] + 1.0
+    )
+    return boxes[0] * (1.0 / 64.0), boxes[1] * (1.0 / 64.0), coherence
+
+
+def store_kernel(
+    inter_ref, coherence_ref, windows, running, inter_out, coherence_out, inter, coherence, sems
+):
+    early, bins = inter_ref.shape[1], inter_out.shape[1]
+    groups = (bins - early) // ROWS
+
+    def copies(source, other, start, count, rows, number):
+        return (
+            pltpu.make_async_copy(
+                source.at[:, pl.ds(rows, count), :],
+                inter_out.at[:, pl.ds(start, count), :],
+                sems.at[0, number],
+            ),
+            pltpu.make_async_copy(
+                other.at[pl.ds(rows, count), :],
+                coherence_out.at[pl.ds(start, count), :],
+                sems.at[1, number],
+            ),
+        )
+
+    pending = [copies(inter_ref, coherence_ref, 0, early, 0, groups)]
+    for group in range(groups):
+        pending.append(
+            copies(inter, coherence, early + group * ROWS, ROWS, group * ROWS, group)
+        )
+    for copy in pending[0]:
         copy.start()
-    for copy in copies:
-        copy.wait()
+    for group in range(groups):
+        now, then = (
+            [windows[part, start : start + ROWS, :] for part in range(4)]
+            for start in (early + group * ROWS, early + (group + 1) * ROWS)
+        )
+        if group == groups - 1:
+            now = [now[part] + running[part] for part in range(4)]
+        if group == groups - 2:
+            then = [then[part] + running[part] for part in range(4)]
+        rows = slice(group * ROWS, (group + 1) * ROWS)
+        inter[0, rows, :], inter[1, rows, :], coherence[rows, :] = results(now, then)
+        if group > 0:
+            for copy in pending[group]:
+                copy.start()
+    for copy in pending[groups]:
+        copy.start()
+    for pair in pending:
+        for copy in pair:
+            copy.wait()
 
 
 def fits(parts, lines_count, range_count):
@@ -963,7 +1000,7 @@
         return staged_on_device(raw_first, raw_second, offsets, chirp_lengths)
     lines = parts * lines_count
     bins = WINDOW // parts
-    groups, halves = bins // ROWS, lines_count // TILE
+    groups, early = bins // ROWS, bins - 3 * ROWS
     taps = min(range_count, lines) // 4 // TILE + 1
     depth = (taps + 1) * TILE
     left, right, twist = host_tables(lines)
@@ -976,11 +1013,13 @@
     held = pl.pallas_call(
         functools.partial(fused_kernel, parts, taps),
         out_shape=(
-            pltpu.VMEM((2, bins, lines), jnp.float32),
-            pltpu.VMEM((bins, lines), jnp.float32),
+            pltpu.VMEM((2, early, lines), jnp.float32),
+            pltpu.VMEM((early, lines), jnp.float32),
+            pltpu.VMEM((4, bins + ROWS, lines), jnp.float32),
+            pltpu.VMEM((4, ROWS, lines), jnp.float32),
         ),
         in_specs=[smem, smem, hbm, hbm, vmem, vmem, vmem],
-        out_specs=(vmem, vmem),
+        out_specs=(vmem, vmem, vmem, vmem),
         scratch_shapes=[
             pltpu.VMEM((2, lines_count, WINDOW - TILE + depth), jnp.bfloat16),
             pltpu.VMEM((4, depth, 2 * TILE), jnp.bfloat16),
@@ -991,23 +1030,21 @@
             got,
             got,
             pltpu.VMEM((2, bins + ROWS, lines), jnp.float32),
-            pltpu.VMEM((4, bins + ROWS, lines), jnp.float32),
-            pltpu.VMEM((4, ROWS, lines), jnp.float32),
+            pltpu.VMEM((bins + ROWS, lines), jnp.float32),
             pltpu.VMEM((2, 4, ROWS, lines), jnp.float32),
             pltpu.VMEM((2, 16, lines), jnp.float32),
             pltpu.VMEM((2, 16, lines), jnp.float32),
-            dma((halves,)),
-            dma((halves, parts)),
-            dma((halves, parts)),
-            dma((groups, parts)),
-            dma((groups, parts)),
+            dma((lines_count // LANES,)),
+            dma((2,)),
+            dma((groups,)),
+            dma((groups,)),
             dma((2, 2)),
             dma((2, parts)),
             dma((2,)),
             dma((2,)),
         ],
         compiler_params=pltpu.CompilerParams(
-            collective_id=0, has_side_effects=True, vmem_limit_bytes=57 * 1024 * 1024
+            collective_id=0, has_side_effects=True, vmem_limit_bytes=49 * 1024 * 1024
         ),
         name="fused",
     )(offsets, chirp_lengths, raw_first, raw_second, left, right, twist)
@@ -1017,10 +1054,14 @@
             jax.ShapeDtypeStruct((2, bins, lines), jnp.float32),
             jax.ShapeDtypeStruct((bins, lines), jnp.float32),
         ),
-        in_specs=[vmem, vmem],
+        in_specs=[vmem, vmem, vmem, vmem],
         out_specs=(hbm, hbm),
-        scratch_shapes=[dma((2,))],
-        compiler_params=pltpu.CompilerParams(vmem_limit_bytes=1024 * 1024),
+        scratch_shapes=[
+            pltpu.VMEM((2, bins - early, lines), jnp.float32),
+            pltpu.VMEM((bins - early, lines), jnp.float32),
+            dma((2, 4)),
+        ],
+        compiler_params=pltpu.CompilerParams(vmem_limit_bytes=8 * 1024 * 1024),
         name="store",
     )(*held)
 

time: 204 us -> 197 us (0.966)
  Pallas kernels: 203 us -> 196 us
    pallas_call x1, Pallas kernels: 201 us -> 193 us  [on_device(): pl.pallas_call(functools.partial(fused_kernel, parts, taps), out_shape=(p...]
where the time goes in v3:
time: 197 us
  Pallas kernels  196 us (99%)
    pallas_call x1, Pallas kernels, on_device(): pl.pallas_call(functools.partial(fused_kernel, parts, taps), out_shape=(p...  193 us

profile of v3, /device:TPU:15, one launch (start us, length us, event | category | flops | bytes accessed | tf_op | source)
XLA Modules:
  0.0 196.8 jit_solution(133311426687520279)
XLA Ops:
  0.6 193.4 %fused.1 = (f32[2,40,8192]{2,1,0:T(8,128)S(1)}, f32[40,8192]{1,0:T(8,128)S(1)}, f32[4,72,8192]{2,1,0:T(8,128)S(1)}, f32[4,8,8192]{2,1,0:T(8,128)S(1)}) custom-call(s32[2]{0:T(128)} %offset_ref.1, s32[2]{0:T(128)} %length_ref.1, bf16[2,512,8192]{2,1,0:T(8,128)(2,1)} %raw_first.1, bf16[2,512,8192]{2,1,0:T(8,128)(2,1)} %raw_second.1, ...), custom_call_target="tpu_custom_call" | custom-call | tf_op jit(solution)/shard_map/fused/pallas_call | solution.py:1013
  194.1 2.7 %store.1 = (f32[2,64,8192]{2,1,0:T(8,128)}, f32[64,8192]{1,0:T(8,128)}) custom-call(f32[2,40,8192]{2,1,0:T(8,128)S(1)} %get-tuple-element.6.inter_ref, f32[40,8192]{1,0:T(8,128)S(1)} %get-tuple-element.7.coherence_ref, f32[4,72,8192]{2,1,0:T(8,128)S(1)} %get-tuple-element.8.windows, f32[4,8,8192]{2,1,0:T(8,128)S(1)} %get-tuple-element.9.running), custom_call_target="tpu_custom_call" | custom-call | tf_op jit(solution)/shard_map/store/pallas_call | solution.py:1051

commit v4 on v3

--- a/solution.py
+++ b/solution.py
@@ -587,7 +587,6 @@
     lax.fori_loop(1, parts, greet, 0)
     raw[:, :, 0:LANES] = jnp.zeros((2, lines_count, LANES), jnp.bfloat16)
     build_table(taps, 0, length_ref[0], seg, tab)
-    pl.semaphore_wait(barrier, parts - 1)
 
     half = me // (parts // 2)
     turn = lax.rem(me // per_block, blocks // 2)
@@ -642,6 +641,10 @@
 
         correlate(block, piece, LANES, LANES, taps * TILE, sent_first, None)
 
+        @pl.when(step == 0)
+        def _():
+            pl.semaphore_wait(barrier, parts - 1)
+
         def send(item, inner):
             dest = block * per_block + lax.rem(item + me, per_block)
 
@@ -661,10 +664,10 @@
 
     def halo_copy(number, side, source):
         sent, got = ((sent_first, got_first), (sent_second, got_second))[number]
-        owner, start, place = ((middle, ROWS, 0), (middle - 1, ROWS // 2, ROWS // 2))[side]
+        owner, start, place, count = ((middle, ROWS, 0, 4), (middle - 1, 5, 5, 3))[side]
         return pltpu.make_async_remote_copy(
-            src_ref=sent.at[owner, :, pl.ds(start, ROWS // 2), :],
-            dst_ref=got.at[source, :, pl.ds(bins + place, ROWS // 2), :],
+            src_ref=sent.at[owner, :, pl.ds(start, count), :],
+            dst_ref=got.at[source, :, pl.ds(bins + place, count), :],
             send_sem=halo_send.at[number, side],
             recv_sem=halo_recv.at[number, source],
             device_id={"az": middle - 1 + side},
@@ -677,15 +680,13 @@
             def _():
                 halo_copy(number, side, me).start()
 
-        half_rows = ROWS // 2
-
         @pl.when(me == middle - 1)
         def _():
-            got[me, :, bins : bins + half_rows, :] = sent[middle, :, ROWS : ROWS + half_rows, :]
+            got[me, :, bins : bins + 4, :] = sent[middle, :, ROWS : ROWS + 4, :]
 
         @pl.when(me == middle)
         def _():
-            got[me, :, bins + half_rows : bins + ROWS, :] = sent[middle - 1, :, half_rows:ROWS, :]
+            got[me, :, bins + 5 : bins + ROWS, :] = sent[middle - 1, :, 5:ROWS, :]
 
     def halo_arrived(number):
         for side in range(2):

time: 197 us -> 196 us (level)
  no operation moved by 1% of the time
where the time goes in v4:
time: 196 us
  Pallas kernels  195 us (99%)
    pallas_call x1, Pallas kernels, on_device(): pl.pallas_call(functools.partial(fused_kernel, parts, taps), out_shape=(p...  193 us

profile of v4, /device:TPU:15, one launch (start us, length us, event | category | flops | bytes accessed | tf_op | source)
XLA Modules:
  0.0 196.0 jit_solution(13866045847215789719)
XLA Ops:
  0.6 192.7 %fused.1 = (f32[2,40,8192]{2,1,0:T(8,128)S(1)}, f32[40,8192]{1,0:T(8,128)S(1)}, f32[4,72,8192]{2,1,0:T(8,128)S(1)}, f32[4,8,8192]{2,1,0:T(8,128)S(1)}) custom-call(s32[2]{0:T(128)} %offset_ref.1, s32[2]{0:T(128)} %length_ref.1, bf16[2,512,8192]{2,1,0:T(8,128)(2,1)} %raw_first.1, bf16[2,512,8192]{2,1,0:T(8,128)(2,1)} %raw_second.1, ...), custom_call_target="tpu_custom_call" | custom-call | tf_op jit(solution)/shard_map/fused/pallas_call | solution.py:1014
  193.3 2.7 %store.1 = (f32[2,64,8192]{2,1,0:T(8,128)}, f32[64,8192]{1,0:T(8,128)}) custom-call(f32[2,40,8192]{2,1,0:T(8,128)S(1)} %get-tuple-element.6.inter_ref, f32[40,8192]{1,0:T(8,128)S(1)} %get-tuple-element.7.coherence_ref, f32[4,72,8192]{2,1,0:T(8,128)S(1)} %get-tuple-element.8.windows, f32[4,8,8192]{2,1,0:T(8,128)S(1)} %get-tuple-element.9.running), custom_call_target="tpu_custom_call" | custom-call | tf_op jit(solution)/shard_map/store/pallas_call | solution.py:1052
